TPU v7x, 32 devices: a whole 2x2x4 slice. The times are simulated.
32 devices in a mesh: batch: 2 (over x), w: 4 (over z), h: 4 (over y, core).
Axes of the slice: x: 2, y: 2, z: 4, core: 2. Of those that a mesh axis runs over, the one named last changes fastest.
Arguments:
- images: bfloat16 [32, 1024, 512, 4], P('batch', 'h', 'w'), parts along dimension 0
- down_w1: bfloat16 [3, 3, 4, 32], replicated
- down_b1: float32 [32], replicated
- refine_w1: bfloat16 [3, 3, 32, 32], replicated
- refine_b1: float32 [32], replicated
- down_w2: bfloat16 [3, 3, 32, 64], replicated
- down_b2: float32 [64], replicated
- refine_w2: bfloat16 [3, 3, 64, 64], replicated
- refine_b2: float32 [64], replicated
- down_w3: bfloat16 [3, 3, 64, 128], replicated
- down_b3: float32 [128], replicated
- refine_w3: bfloat16 [3, 3, 128, 128], replicated
- refine_b3: float32 [128], replicated
Outputs:
- output: bfloat16 [32, 128, 64, 128], P('batch', 'h', 'w'), parts along dimension 0
There are 2 independent parts. A program takes and returns all parts, laid end to end along the dimension named above; an argument that names none is the same for every part.
All inputs are finite; a program needn't handle non-finite values.
Results may differ from a plain program's by a relative error of at most 0.00187565.
Values are sent between devices in bfloat16 or wider.
A program may use at most 1 GiB of HBM per device.

v0:
```python
import functools

import jax
import jax.numpy as jnp
import numpy as np
from jax import lax
from jax.experimental import pallas as pl
from jax.experimental.pallas import tpu as pltpu
from jax.sharding import PartitionSpec as P

BF = jnp.bfloat16
F32 = jnp.float32
N = 16
G = 16
MESH = pl.DeviceIdType.MESH


def first_weight_selector():
    sel = np.zeros((8, 256, 36), np.float32)
    for j in range(8):
        for c in range(4):
            for wi in range(16):
                b = wi - 2 * j + 1
                if 0 <= b <= 2:
                    for hi in range(2):
                        sel[j, hi * 64 + c * 16 + wi, ((hi + 1) * 3 + b) * 4 + c] = 1
                    sel[j, 128 + 64 + c * 16 + wi, (0 * 3 + b) * 4 + c] = 1
            if j == 0:
                for a, wi in ((1, 15), (2, 14), (0, 13)):
                    sel[j, 128 + c * 16 + wi, (a * 3) * 4 + c] = 1
    return sel.reshape(8 * 256, 36)


def roll(v, shift):
    shift %= 128
    return v if shift == 0 else pltpu.roll(v, shift, v.ndim - 1)


def flat(v):
    return v.reshape(-1, 128)


def build_weight(big, w, k_blocks, stride):
    cin, cout = w.shape[2], w.shape[3]
    ncols = 128 // cout
    zero = jnp.zeros((cin, cout), BF)
    for kp, pos in enumerate(k_blocks):
        for orow in range(2):
            pieces = []
            for j in range(ncols):
                piece = zero
                if pos is not None:
                    a, b = pos[0] - stride * orow, pos[1] - stride * j + 1
                    if 0 <= a <= 2 and 0 <= b <= 2:
                        piece = w[a, b]
                pieces.append(piece)
            big[kp * cin:(kp + 1) * cin, orow * 128:(orow + 1) * 128] = (
                pieces[0] if ncols == 1 else jnp.concatenate(pieces, axis=1))


REFINE1_K = ([(ir, ic) for ir in range(4) for ic in range(4)]
             + [p for e in (0, 2) for p in ((e, 4), (e + 1, -1), (e + 1, 4), (e, -1))])
REFINE2_K = ([(ir, ic) for ir in range(4) for ic in range(2)]
             + [p for ir in range(4) for p in ((ir, 2), (ir, -1))])
REFINE3_K = [(ir, ic) for ir in range(4) for ic in (-1, 0, 1)]
DOWN2_K = ([(ir, ic) for ir in range(5) for ic in range(4)]
           + [p for e in (0, 2) for p in (None, (e + 1, -1), None, (e, -1))]
           + [None, None, None, (4, -1)])
DOWN3_K = ([(ir, ic) for ir in range(5) for ic in range(2)]
           + [p for e in (0, 2) for p in ((e + 1, -1), (e, -1))] + [None, (4, -1)])


def tiled_bias(b):
    reps = 128 // b.shape[1]
    return jnp.concatenate([b[...]] * (2 * reps), axis=1)


def emit(res, bias, dst, row0, pairs, g0, ng):
    val = jnp.maximum(res + bias, 0.0).astype(BF).reshape(pairs, ng, N, 256)
    for p in range(pairs):
        for half in range(2):
            dst(row0 + 2 * p + half, g0, ng, val[p, :, :, half * 128:(half + 1) * 128])


def refine_lhs(stage, src, row0, g0, ng):
    def own(h):
        return flat(src[row0 + h, pl.ds(1 + g0, ng)])

    def left(h):
        return flat(src[row0 + h, pl.ds(g0, ng)])

    def right(h):
        return flat(src[row0 + h, pl.ds(2 + g0, ng)])

    def edge(h):
        return jnp.concatenate([right(h)[:, :64], left(h)[:, 64:]], axis=1)

    if stage == 3:
        return [f(h) for h in range(4) for f in (left, own, right)]
    if stage == 2:
        return [own(h) for h in range(4)] + [edge(h) for h in range(4)]
    ks = [own(h) for h in range(4)]
    for h in (0, 2):
        f0, f1 = edge(h), roll(edge(h + 1), 64)
        ks.append(jnp.concatenate([f0[:, :32], f1[:, 32:96], f0[:, 96:]], axis=1))
    return ks


def down_lhs(src, row0, g0, ng):
    def own(h):
        return flat(src[2 * row0 + h, pl.ds(1 + g0, ng)])

    def left(h):
        return flat(src[2 * row0 + h, pl.ds(g0, ng)])

    ks = [own(h) for h in range(5)]
    for h in (0, 2):
        ks.append(jnp.concatenate([roll(left(h + 1), 64)[:, :64], left(h)[:, 64:]], axis=1))
    return ks + [left(4)]


def conv_rows(lhs, weight, bias, dst, row_lo, row_hi, g0, ng, pairs):
    steps = (row_hi - row_lo) // (2 * pairs)

    def step(i, carry):
        row0 = row_lo + i * (2 * pairs)
        per_pair = [lhs(row0 + 2 * p, g0, ng) for p in range(pairs)]
        ks = [jnp.concatenate(part, axis=0) if pairs > 1 else part[0] for part in zip(*per_pair)]
        res = jnp.dot(jnp.concatenate(ks, axis=1), weight[...], preferred_element_type=F32)
        emit(res, bias, dst, row0, pairs, g0, ng)
        return carry

    lax.fori_loop(0, steps, step, 0)


def pack_cols(stage, buf, rows, right_edge):
    col = buf[pl.ds(1, rows), G if right_edge else 1]
    per = 4 if stage == 1 else 2
    width = 128 // per
    col = col.reshape(rows // per, per, N, 128)
    base = 128 - width if right_edge else 0
    parts = []
    for k in range(per):
        v = roll(flat(col[:, k]), k * width - base)
        parts.append(v[:, k * width:(k + 1) * width])
    return jnp.concatenate(parts, axis=1).reshape(rows // per, N, 128)


def unpack_cols(stage, buf, rows, packed, left_halo):
    per = 4 if stage == 1 else 2
    width = 128 // per
    base = 128 - width if left_halo else 0
    g = 0 if left_halo else G + 1
    for k in range(per):
        v = roll(flat(packed[...]), base - k * width).reshape(rows // per, N, 128)
        for i in range(rows // per):
            buf[1 + i * per + k, g] = v[i]


def kernel(h_count, w_count, rows1, x, sel, dw1, db1, rw1, rb1, dw2, db2, rw2, rb2, dw3, db3, rw3, rb3, out,
           pv, y1, z1, y2, z2, y3, bw1, br1, bw2, br2, bw3, br3,
           send_x, recv_x, send_c, recv_c, send_sem, recv_sem):
    rows2, rows3 = rows1 // 2, rows1 // 4
    me_h, me_w = lax.axis_index('h'), lax.axis_index('w')

    def device(dh, dw):
        return {'h': lax.rem(me_h + dh + h_count, h_count), 'w': lax.rem(me_w + dw + w_count, w_count)}

    barrier = pltpu.get_barrier_semaphore()
    others = [(dh, dw) for dh in (-1, 0, 1) for dw in (-1, 0, 1) if dh or dw]
    for dh, dw in others:
        pl.semaphore_signal(barrier, inc=1, device_id=device(dh, dw), device_id_type=MESH)

    def copies(e, buf, rows, ng, both, send_col, recv_col):
        last = rows
        table = [
            (buf.at[last, pl.ds(1, ng)], buf.at[0, pl.ds(1, ng)], (1, 0)),
            (send_col[0], recv_col[0], (0, 1)),
            (buf.at[last, ng], buf.at[0, 0], (1, 1)),
        ]
        if both:
            table += [
                (buf.at[1, pl.ds(1, ng)], buf.at[last + 1, pl.ds(1, ng)], (-1, 0)),
                (send_col[1], recv_col[1], (0, -1)),
                (buf.at[last, 1], buf.at[0, ng + 1], (1, -1)),
                (buf.at[1, ng], buf.at[last + 1, 0], (-1, 1)),
                (buf.at[1, 1], buf.at[last + 1, ng + 1], (-1, -1)),
            ]
        return [
            pltpu.make_async_remote_copy(
                src_ref=src, dst_ref=dst, send_sem=send_sem.at[e, d], recv_sem=recv_sem.at[e, d],
                device_id=device(*direction), device_id_type=MESH)
            for d, (src, dst, direction) in enumerate(table)
        ]

    def exchange(e, stage, buf, rows, both):
        if stage == 3:
            send_col = [buf.at[pl.ds(1, rows), G], buf.at[pl.ds(1, rows), 1]]
            recv_col = [buf.at[pl.ds(1, rows), 0], buf.at[pl.ds(1, rows), G + 1]]
        else:
            send_col = [send_c.at[e, 0], send_c.at[e, 1]]
            recv_col = [recv_c.at[e, 0], recv_c.at[e, 1]]
            send_c[e, 0] = pack_cols(stage, buf, rows, True)
            if both:
                send_c[e, 1] = pack_cols(stage, buf, rows, False)
        todo = copies(e, buf, rows, G, both, send_col, recv_col)
        for c in todo:
            c.start()
        for c in todo:
            c.wait()
        if stage != 3:
            unpack_cols(stage, buf, rows, recv_c.at[e, 0], True)
            if both:
                unpack_cols(stage, buf, rows, recv_c.at[e, 1], False)

    picked = jnp.dot(sel[...], dw1[...], preferred_element_type=F32).astype(BF)
    bw1[...] = jnp.concatenate([picked[j * 256:(j + 1) * 256] for j in range(8)], axis=1)
    build_weight(br1, rw1, REFINE1_K, 1)
    build_weight(bw2, dw2, DOWN2_K, 2)
    build_weight(br2, rw2, REFINE2_K, 1)
    build_weight(bw3, dw3, DOWN3_K, 2)
    build_weight(br3, rw3, REFINE3_K, 1)

    lane = lax.broadcasted_iota(jnp.int16, (N, 128), 1)

    def swap(v, dist, blocks):
        mask = (lane & dist) == 0
        new = list(v)
        for i in range(8):
            if not i & blocks:
                a, b = v[i], v[i + blocks]
                new[i] = jnp.where(mask, a, roll(b, dist))
                new[i + blocks] = jnp.where(mask, roll(a, -dist), b)
        return new

    def to_pairs(i, carry):
        t = jnp.transpose(x[:, pl.ds(i * 16, 16), :], (1, 0, 2))
        for p in range(2):
            v = [t[p * 8 + k] for k in range(8)]
            for dist, blocks in ((64, 4), (32, 2), (16, 1)):
                v = swap(v, dist, blocks)
            for q in range(8):
                pv[1 + 2 * i + p, 1 + q] = v[q]
        return carry

    lax.fori_loop(0, rows1 // 2, to_pairs, 0)

    pl.semaphore_wait(barrier, len(others))

    lanes = lax.broadcasted_iota(jnp.int16, (rows1, 128), 1) & 15
    col = pv[pl.ds(1, rows1), 8].reshape(rows1 // 16, 16, N, 128)
    packed = flat(col[:, 15])
    for k in range(15):
        packed = jnp.where(lanes == k, roll(flat(col[:, k]), k - 15), packed)
    send_x[...] = packed.reshape(rows1 // 16, N, 128)
    todo = copies(0, pv, rows1, 8, False, [send_x], [recv_x])
    for c in todo:
        c.start()
    for c in todo:
        c.wait()
    for k in range(16):
        v = roll(flat(recv_x[...]), 15 - k).reshape(rows1 // 16, N, 128)
        for i in range(rows1 // 16):
            pv[1 + 16 * i + k, 0] = v[i]

    bias1 = tiled_bias(db1)
    per = 4

    def down1(i, carry):
        row0 = i * per
        size = per * 8 * N
        sub = lax.broadcasted_iota(jnp.int16, (size, 128), 1) & 15
        own = flat(pv[pl.ds(row0 + 1, per), pl.ds(1, 8)])
        above = flat(pv[pl.ds(row0, per), pl.ds(1, 8)])
        left = flat(pv[pl.ds(row0 + 1, per), pl.ds(0, 8)])
        above_left = flat(pv[pl.ds(row0, per), pl.ds(0, 8)])
        edge = jnp.where(sub == 15, left, jnp.where(sub == 14, roll(left, 63), roll(above_left, 62)))
        second = jnp.concatenate([edge[:, :64], above[:, 64:]], axis=1)
        res = jnp.dot(jnp.concatenate([own, second], axis=1), bw1[...], preferred_element_type=F32)
        val = jnp.maximum(res + bias1, 0.0).astype(BF).reshape(per, 8, N, 256)
        for r in range(per):
            for q in range(8):
                y1[row0 + 1 + r, 1 + 2 * q] = val[r, q, :, :128]
                y1[row0 + 1 + r, 2 + 2 * q] = val[r, q, :, 128:]
        return carry

    lax.fori_loop(0, rows1 // per, down1, 0)

    def into(buf):
        def dst(row, g0, ng, val):
            buf[row + 1, pl.ds(1 + g0, ng)] = val
        return dst

    def into_out(row, g0, ng, val):
        out[row, pl.ds(g0, ng)] = val

    exchange(1, 1, y1, rows1, True)
    conv_rows(functools.partial(refine_lhs, 1, y1), br1, tiled_bias(rb1), into(z1), 0, rows1, 0, G, 2)
    exchange(2, 1, z1, rows1, False)
    conv_rows(functools.partial(down_lhs, z1), bw2, tiled_bias(db2), into(y2), 0, rows2, 0, G, 2)
    exchange(3, 2, y2, rows2, True)
    conv_rows(functools.partial(refine_lhs, 2, y2), br2, tiled_bias(rb2), into(z2), 0, rows2, 0, G, 2)
    exchange(4, 2, z2, rows2, False)
    conv_rows(functools.partial(down_lhs, z2), bw3, tiled_bias(db3), into(y3), 0, rows3, 0, G, 2)
    exchange(5, 3, y3, rows3, True)
    conv_rows(functools.partial(refine_lhs, 3, y3), br3, tiled_bias(rb3), into_out, 0, rows3, 0, G, 2)


def encode(h_count, w_count, images, *params):
    rows1 = images.shape[1] // 2
    rows2, rows3 = rows1 // 2, rows1 // 4
    x = jnp.transpose(images, (0, 1, 3, 2)).reshape(N, rows1 * 8, 128)
    args = [x, jnp.asarray(first_weight_selector(), BF)]
    for i, p in enumerate(params):
        args.append(p.reshape(1, -1) if i % 2 else (p.reshape(36, 32) if i == 0 else p))

    def act(rows, groups):
        return pltpu.VMEM((rows, groups, N, 128), BF)

    flops = 2 * 16 * rows1 * 64 * 32 * 9 * (4 + 32 + 16 + 32 + 16 + 32)
    out = pl.pallas_call(
        functools.partial(kernel, h_count, w_count, rows1),
        name='encoder',
        out_shape=jax.ShapeDtypeStruct((rows3, G, N, 128), BF),
        in_specs=[pl.BlockSpec(memory_space=pltpu.VMEM)] * len(args),
        out_specs=pl.BlockSpec(memory_space=pltpu.VMEM),
        scratch_shapes=[
            act(rows1 + 1, 9), act(rows1 + 2, G + 2), act(rows1 + 1, G + 1),
            act(rows2 + 2, G + 2), act(rows2 + 1, G + 1), act(rows3 + 2, G + 2),
            pltpu.VMEM((256, 256), BF), pltpu.VMEM((768, 256), BF), pltpu.VMEM((1024, 256), BF),
            pltpu.VMEM((1024, 256), BF), pltpu.VMEM((1024, 256), BF), pltpu.VMEM((1536, 256), BF),
            pltpu.VMEM((rows1 // 16, N, 128), BF), pltpu.VMEM((rows1 // 16, N, 128), BF),
            pltpu.VMEM((5, 2, rows1 // 4, N, 128), BF), pltpu.VMEM((5, 2, rows1 // 4, N, 128), BF),
            pltpu.SemaphoreType.DMA((6, 8)), pltpu.SemaphoreType.DMA((6, 8)),
        ],
        compiler_params=pltpu.CompilerParams(
            collective_id=0, has_side_effects=True, vmem_limit_bytes=67043328),
        cost_estimate=pl.CostEstimate(flops=flops, bytes_accessed=7 * 2**20, transcendentals=0),
    )(*args)
    return jnp.transpose(out, (2, 0, 1, 3))


def solution(mesh):
    tile_spec = P('batch', 'h', 'w', None)
    body = functools.partial(encode, mesh.shape['h'], mesh.shape['w'])
    return jax.shard_map(body, mesh=mesh, in_specs=(tile_spec,) + (P(),) * 12, out_specs=tile_spec, check_vma=False)
```

profile of v0, /device:TPU:0, one launch (start us, length us, event | category | flops | bytes accessed | tf_op | source)
XLA Modules:
  0.0 116.9 jit_solution(17213034002340111344)
XLA Ops:
  0.0 1.3 %reshape.25.dw1 = bf16[36,32]{1,0:T(8,128)(2,1)} reshape(bf16[3,3,4,32]{3,2,1,0:T(4,128)(2,1)} %param.15) | data formatting | bytes 4608 | tf_op jit(solution)/shard_map/reshape | solution.py:315
  1.3 112.1 %encoder.1 = bf16[32,16,16,128]{3,2,1,0:T(8,128)(2,1)} custom-call(bf16[16,1024,128]{2,1,0:T(8,128)(2,1)} %bitcast.11, bf16[2048,36]{1,0:T(8,128)(2,1)} %constant.2.clone.sel, bf16[36,32]{1,0:T(8,128)(2,1)} %reshape.25.dw1, f32[1,32]{1,0:T(1,128)} %bitcast.12, bf16[3,3,32,32]{3,2,1,0:T(8,128)(2,1)} %rw1.1, f32[1,32]{1,0:T(1,128)} %bitcast.13, ...), custom_call_target="tpu_custom_call" | custom-call | flops 9965666304 | bytes 7340032 | tf_op jit(solution)/shard_map/encoder/pallas_call | solution.py:321
  113.5 3.5 %copy.16 = bf16[16,32,16,128]{3,2,1,0:T(8,128)(2,1)} copy(bf16[16,32,16,128]{3,0,2,1:T(8,128)(2,1)} %bitcast.10) | data formatting | bytes 4194304 | tf_op jit(solution)/shard_map/transpose | solution.py:340
where the time goes:
time: 118 us; the launch traced here: 117 us
  Pallas kernels  112 us (95%)
  local copies, waits for them, and re-layouts  4.77 us (4%)
    pallas_call x1, Pallas kernels, encode(): pl.pallas_call(functools.partial(kernel, h_count, w_count, rows1), name='...  112 us
    transpose x1, local copies, waits for them, and re-layouts, encode(): return jnp.transpose(out, (2, 0, 1, 3))  3.45 us

commit v1 on v0

--- a/solution.py
+++ b/solution.py
@@ -133,8 +133,9 @@
     lax.fori_loop(0, steps, step, 0)
 
 
-def pack_cols(stage, buf, rows, right_edge):
-    col = buf[pl.ds(1, rows), G if right_edge else 1]
+def pack_cols(stage, buf, lo, hi, right_edge):
+    rows = hi - lo
+    col = buf[pl.ds(1 + lo, rows), G if right_edge else 1]
     per = 4 if stage == 1 else 2
     width = 128 // per
     col = col.reshape(rows // per, per, N, 128)
@@ -146,22 +147,126 @@
     return jnp.concatenate(parts, axis=1).reshape(rows // per, N, 128)
 
 
-def unpack_cols(stage, buf, rows, packed, left_halo):
+def unpack_cols(stage, buf, lo, hi, packed, left_halo):
     per = 4 if stage == 1 else 2
     width = 128 // per
     base = 128 - width if left_halo else 0
     g = 0 if left_halo else G + 1
+    tiles = flat(packed)
     for k in range(per):
-        v = roll(flat(packed[...]), base - k * width).reshape(rows // per, N, 128)
-        for i in range(rows // per):
-            buf[1 + i * per + k, g] = v[i]
-
-
-def kernel(h_count, w_count, rows1, x, sel, dw1, db1, rw1, rb1, dw2, db2, rw2, rb2, dw3, db3, rw3, rb3, out,
-           pv, y1, z1, y2, z2, y3, bw1, br1, bw2, br2, bw3, br3,
-           send_x, recv_x, send_c, recv_c, send_sem, recv_sem):
+        v = roll(tiles, base - k * width).reshape(-1, N, 128)
+        for i in range((hi - lo) // per):
+            buf[1 + lo + i * per + k, g] = v[i]
+
+
+def pack_image(pv, lo, hi):
+    rows = hi - lo
+    col = pv[pl.ds(1 + lo, rows), 8].reshape(rows // 16, 16, N, 128)
+    lanes = lax.broadcasted_iota(jnp.int16, (rows, 128), 1) & 15
+    packed = flat(col[:, 15])
+    for k in range(15):
+        packed = jnp.where(lanes == k, roll(flat(col[:, k]), k - 15), packed)
+    return packed.reshape(rows // 16, N, 128)
+
+
+def unpack_image(pv, lo, hi, packed):
+    tiles = flat(packed)
+    for k in range(16):
+        v = roll(tiles, 15 - k).reshape(-1, N, 128)
+        for i in range((hi - lo) // 16):
+            pv[1 + lo + 16 * i + k, 0] = v[i]
+
+
+def row_blocks(rows, start, size):
+    out = [(lo, min(lo + size, rows)) for lo in range(start, rows, size)]
+    return out + [(lo, min(lo + size, start)) for lo in range(0, start, size)]
+
+
+class Halo:
+    def __init__(self, stage, buf, rows, groups, both, send_c, recv_c, sems, device):
+        self.stage, self.buf, self.rows, self.groups, self.both = stage, buf, rows, groups, both
+        self.send_c, self.recv_c, self.sems, self.device = send_c, recv_c, sems, device
+        self.count, self.sent, self.chunks, self.top, self.bottom = 0, [], [], [], []
+
+    def copy(self, src, dst, direction):
+        send_sem, recv_sem = self.sems
+        c = pltpu.make_async_remote_copy(
+            src_ref=src, dst_ref=dst, send_sem=send_sem.at[self.count], recv_sem=recv_sem.at[self.count],
+            device_id=self.device(*direction), device_id_type=MESH)
+        self.count += 1
+        self.sent.append(c)
+        c.start()
+        return c
+
+    def send(self, lo, hi):
+        buf, last, ng, stage = self.buf, self.rows, self.groups, self.stage
+        got = []
+        for side in range(2 if self.both else 1):
+            direction = (0, 1) if side == 0 else (0, -1)
+            if stage == 3:
+                src = buf.at[pl.ds(1 + lo, hi - lo), G if side == 0 else 1]
+                dst = buf.at[pl.ds(1 + lo, hi - lo), 0 if side == 0 else G + 1]
+            else:
+                per = {0: 16, 1: 4, 2: 2}[stage]
+                part = pl.ds(lo // per, (hi - lo) // per)
+                self.send_c[side, part] = (
+                    pack_image(buf, lo, hi) if stage == 0 else pack_cols(stage, buf, lo, hi, side == 0))
+                src, dst = self.send_c.at[side, part], self.recv_c.at[side, part]
+            got.append(self.copy(src, dst, direction))
+        self.chunks.append((lo, hi, got))
+        if hi == self.rows:
+            self.top.append(self.copy(buf.at[last, pl.ds(1, ng)], buf.at[0, pl.ds(1, ng)], (1, 0)))
+            self.top.append(self.copy(buf.at[last, ng], buf.at[0, 0], (1, 1)))
+            if self.both:
+                self.top.append(self.copy(buf.at[last, 1], buf.at[0, ng + 1], (1, -1)))
+        if lo == 0 and self.both:
+            self.bottom.append(self.copy(buf.at[1, pl.ds(1, ng)], buf.at[last + 1, pl.ds(1, ng)], (-1, 0)))
+            self.bottom.append(self.copy(buf.at[1, ng], buf.at[last + 1, 0], (-1, 1)))
+            self.bottom.append(self.copy(buf.at[1, 1], buf.at[last + 1, ng + 1], (-1, -1)))
+
+    def need(self, lo, hi):
+        left = []
+        for first, end, got in self.chunks:
+            if first < hi and lo < end:
+                for side, c in enumerate(got):
+                    c.wait_recv()
+                    if self.stage != 3:
+                        per = {0: 16, 1: 4, 2: 2}[self.stage]
+                        packed = self.recv_c[side, pl.ds(first // per, (end - first) // per)]
+                        if self.stage == 0:
+                            unpack_image(self.buf, first, end, packed)
+                        else:
+                            unpack_cols(self.stage, self.buf, first, end, packed, side == 0)
+            else:
+                left.append((first, end, got))
+        self.chunks = left
+        if lo < 0:
+            for c in self.top:
+                c.wait_recv()
+            self.top = []
+        if hi > self.rows:
+            for c in self.bottom:
+                c.wait_recv()
+            self.bottom = []
+
+    def finish(self):
+        assert not (self.chunks or self.top or self.bottom)
+        for c in self.sent:
+            c.wait_send()
+
+
+def kernel(h_count, w_count, rows1, x_hbm, sel, dw1, db1, rw1, rb1, dw2, db2, rw2, rb2, dw3, db3, rw3, rb3, out,
+           x, pv, y1, z1, y2, z2, y3, bw1, br1, bw2, br2, bw3, br3,
+           send_x, recv_x, send_c, recv_c, x_sem, send_sem, recv_sem):
     rows2, rows3 = rows1 // 2, rows1 // 4
     me_h, me_w = lax.axis_index('h'), lax.axis_index('w')
+
+    image_blocks = row_blocks(rows1, 0, 32)
+    loads = []
+    for i, (lo, hi) in enumerate(image_blocks):
+        part = pl.ds(lo * 8, (hi - lo) * 8)
+        loads.append(pltpu.make_async_copy(x_hbm.at[:, part], x.at[:, part], x_sem.at[i]))
+        loads[-1].start()
 
     def device(dh, dw):
         return {'h': lax.rem(me_h + dh + h_count, h_count), 'w': lax.rem(me_w + dw + w_count, w_count)}
@@ -170,48 +275,6 @@
     others = [(dh, dw) for dh in (-1, 0, 1) for dw in (-1, 0, 1) if dh or dw]
     for dh, dw in others:
         pl.semaphore_signal(barrier, inc=1, device_id=device(dh, dw), device_id_type=MESH)
-
-    def copies(e, buf, rows, ng, both, send_col, recv_col):
-        last = rows
-        table = [
-            (buf.at[last, pl.ds(1, ng)], buf.at[0, pl.ds(1, ng)], (1, 0)),
-            (send_col[0], recv_col[0], (0, 1)),
-            (buf.at[last, ng], buf.at[0, 0], (1, 1)),
-        ]
-        if both:
-            table += [
-                (buf.at[1, pl.ds(1, ng)], buf.at[last + 1, pl.ds(1, ng)], (-1, 0)),
-                (send_col[1], recv_col[1], (0, -1)),
-                (buf.at[last, 1], buf.at[0, ng + 1], (1, -1)),
-                (buf.at[1, ng], buf.at[last + 1, 0], (-1, 1)),
-                (buf.at[1, 1], buf.at[last + 1, ng + 1], (-1, -1)),
-            ]
-        return [
-            pltpu.make_async_remote_copy(
-                src_ref=src, dst_ref=dst, send_sem=send_sem.at[e, d], recv_sem=recv_sem.at[e, d],
-                device_id=device(*direction), device_id_type=MESH)
-            for d, (src, dst, direction) in enumerate(table)
-        ]
-
-    def exchange(e, stage, buf, rows, both):
-        if stage == 3:
-            send_col = [buf.at[pl.ds(1, rows), G], buf.at[pl.ds(1, rows), 1]]
-            recv_col = [buf.at[pl.ds(1, rows), 0], buf.at[pl.ds(1, rows), G + 1]]
-        else:
-            send_col = [send_c.at[e, 0], send_c.at[e, 1]]
-            recv_col = [recv_c.at[e, 0], recv_c.at[e, 1]]
-            send_c[e, 0] = pack_cols(stage, buf, rows, True)
-            if both:
-                send_c[e, 1] = pack_cols(stage, buf, rows, False)
-        todo = copies(e, buf, rows, G, both, send_col, recv_col)
-        for c in todo:
-            c.start()
-        for c in todo:
-            c.wait()
-        if stage != 3:
-            unpack_cols(stage, buf, rows, recv_c.at[e, 0], True)
-            if both:
-                unpack_cols(stage, buf, rows, recv_c.at[e, 1], False)
 
     picked = jnp.dot(sel[...], dw1[...], preferred_element_type=F32).astype(BF)
     bw1[...] = jnp.concatenate([picked[j * 256:(j + 1) * 256] for j in range(8)], axis=1)
@@ -220,6 +283,21 @@
     build_weight(br2, rw2, REFINE2_K, 1)
     build_weight(bw3, dw3, DOWN3_K, 2)
     build_weight(br3, rw3, REFINE3_K, 1)
+
+    def halo(e, stage, buf, rows, groups, both):
+        sems = (send_sem.at[e], recv_sem.at[e])
+        if stage == 0:
+            return Halo(stage, buf, rows, groups, both, send_x, recv_x, sems, device)
+        if stage == 3:
+            return Halo(stage, buf, rows, groups, both, None, None, sems, device)
+        return Halo(stage, buf, rows, groups, both, send_c.at[e - 1], recv_c.at[e - 1], sems, device)
+
+    pv_halo = halo(0, 0, pv, rows1, 8, False)
+    y1_halo = halo(1, 1, y1, rows1, G, True)
+    z1_halo = halo(2, 1, z1, rows1, G, False)
+    y2_halo = halo(3, 2, y2, rows2, G, True)
+    z2_halo = halo(4, 2, z2, rows2, G, False)
+    y3_halo = halo(5, 3, y3, rows3, G, True)
 
     lane = lax.broadcasted_iota(jnp.int16, (N, 128), 1)
 
@@ -243,32 +321,19 @@
                 pv[1 + 2 * i + p, 1 + q] = v[q]
         return carry
 
-    lax.fori_loop(0, rows1 // 2, to_pairs, 0)
-
-    pl.semaphore_wait(barrier, len(others))
-
-    lanes = lax.broadcasted_iota(jnp.int16, (rows1, 128), 1) & 15
-    col = pv[pl.ds(1, rows1), 8].reshape(rows1 // 16, 16, N, 128)
-    packed = flat(col[:, 15])
-    for k in range(15):
-        packed = jnp.where(lanes == k, roll(flat(col[:, k]), k - 15), packed)
-    send_x[...] = packed.reshape(rows1 // 16, N, 128)
-    todo = copies(0, pv, rows1, 8, False, [send_x], [recv_x])
-    for c in todo:
-        c.start()
-    for c in todo:
-        c.wait()
-    for k in range(16):
-        v = roll(flat(recv_x[...]), 15 - k).reshape(rows1 // 16, N, 128)
-        for i in range(rows1 // 16):
-            pv[1 + 16 * i + k, 0] = v[i]
+    for i, (lo, hi) in enumerate(image_blocks):
+        loads[i].wait()
+        lax.fori_loop(lo // 2, hi // 2, to_pairs, 0)
+        if i == 0:
+            pl.semaphore_wait(barrier, len(others))
+        pv_halo.send(lo, hi)
 
     bias1 = tiled_bias(db1)
-    per = 4
+    per = 8
+    size = per * 8 * N
 
     def down1(i, carry):
         row0 = i * per
-        size = per * 8 * N
         sub = lax.broadcasted_iota(jnp.int16, (size, 128), 1) & 15
         own = flat(pv[pl.ds(row0 + 1, per), pl.ds(1, 8)])
         above = flat(pv[pl.ds(row0, per), pl.ds(1, 8)])
@@ -284,7 +349,10 @@
                 y1[row0 + 1 + r, 2 + 2 * q] = val[r, q, :, 128:]
         return carry
 
-    lax.fori_loop(0, rows1 // per, down1, 0)
+    for lo, hi in row_blocks(rows1, 8, 32):
+        pv_halo.need(lo - 1, hi)
+        lax.fori_loop(lo // per, hi // per, down1, 0)
+        y1_halo.send(lo, hi)
 
     def into(buf):
         def dst(row, g0, ng, val):
@@ -294,16 +362,27 @@
     def into_out(row, g0, ng, val):
         out[row, pl.ds(g0, ng)] = val
 
-    exchange(1, 1, y1, rows1, True)
-    conv_rows(functools.partial(refine_lhs, 1, y1), br1, tiled_bias(rb1), into(z1), 0, rows1, 0, G, 2)
-    exchange(2, 1, z1, rows1, False)
-    conv_rows(functools.partial(down_lhs, z1), bw2, tiled_bias(db2), into(y2), 0, rows2, 0, G, 2)
-    exchange(3, 2, y2, rows2, True)
-    conv_rows(functools.partial(refine_lhs, 2, y2), br2, tiled_bias(rb2), into(z2), 0, rows2, 0, G, 2)
-    exchange(4, 2, z2, rows2, False)
-    conv_rows(functools.partial(down_lhs, z2), bw3, tiled_bias(db3), into(y3), 0, rows3, 0, G, 2)
-    exchange(5, 3, y3, rows3, True)
-    conv_rows(functools.partial(refine_lhs, 3, y3), br3, tiled_bias(rb3), into_out, 0, rows3, 0, G, 2)
+    def refine(stage, src, src_halo, weight, bias, dst, dst_halo, blocks):
+        for lo, hi in blocks:
+            src_halo.need(lo - 1, hi + 1)
+            conv_rows(functools.partial(refine_lhs, stage, src), weight, bias, dst, lo, hi, 0, G, 2)
+            if dst_halo is not None:
+                dst_halo.send(lo, hi)
+
+    def down(src, src_halo, weight, bias, dst, dst_halo, blocks):
+        for lo, hi in blocks:
+            src_halo.need(2 * lo - 1, 2 * hi)
+            conv_rows(functools.partial(down_lhs, src), weight, bias, dst, lo, hi, 0, G, 2)
+            dst_halo.send(lo, hi)
+
+    refine(1, y1, y1_halo, br1, tiled_bias(rb1), into(z1), z1_halo, row_blocks(rows1, 12, 32))
+    down(z1, z1_halo, bw2, tiled_bias(db2), into(y2), y2_halo, row_blocks(rows2, 8, 16))
+    refine(2, y2, y2_halo, br2, tiled_bias(rb2), into(z2), z2_halo, row_blocks(rows2, 12, 16))
+    down(z2, z2_halo, bw3, tiled_bias(db3), into(y3), y3_halo, row_blocks(rows3, 8, 8))
+    refine(3, y3, y3_halo, br3, tiled_bias(rb3), into_out, None, row_blocks(rows3, 12, 8))
+
+    for h in (pv_halo, y1_halo, z1_halo, y2_halo, z2_halo, y3_halo):
+        h.finish()
 
 
 def encode(h_count, w_count, images, *params):
@@ -322,16 +401,16 @@
         functools.partial(kernel, h_count, w_count, rows1),
         name='encoder',
         out_shape=jax.ShapeDtypeStruct((rows3, G, N, 128), BF),
-        in_specs=[pl.BlockSpec(memory_space=pltpu.VMEM)] * len(args),
+        in_specs=[pl.BlockSpec(memory_space=pl.ANY)] + [pl.BlockSpec(memory_space=pltpu.VMEM)] * (len(args) - 1),
         out_specs=pl.BlockSpec(memory_space=pltpu.VMEM),
         scratch_shapes=[
-            act(rows1 + 1, 9), act(rows1 + 2, G + 2), act(rows1 + 1, G + 1),
+            pltpu.VMEM((N, rows1 * 8, 128), BF), act(rows1 + 1, 9), act(rows1 + 2, G + 2), act(rows1 + 1, G + 1),
             act(rows2 + 2, G + 2), act(rows2 + 1, G + 1), act(rows3 + 2, G + 2),
             pltpu.VMEM((256, 256), BF), pltpu.VMEM((768, 256), BF), pltpu.VMEM((1024, 256), BF),
             pltpu.VMEM((1024, 256), BF), pltpu.VMEM((1024, 256), BF), pltpu.VMEM((1536, 256), BF),
-            pltpu.VMEM((rows1 // 16, N, 128), BF), pltpu.VMEM((rows1 // 16, N, 128), BF),
-            pltpu.VMEM((5, 2, rows1 // 4, N, 128), BF), pltpu.VMEM((5, 2, rows1 // 4, N, 128), BF),
-            pltpu.SemaphoreType.DMA((6, 8)), pltpu.SemaphoreType.DMA((6, 8)),
+            pltpu.VMEM((1, rows1 // 16, N, 128), BF), pltpu.VMEM((1, rows1 // 16, N, 128), BF),
+            pltpu.VMEM((4, 2, rows1 // 4, N, 128), BF), pltpu.VMEM((4, 2, rows1 // 4, N, 128), BF),
+            pltpu.SemaphoreType.DMA((8,)), pltpu.SemaphoreType.DMA((6, 20)), pltpu.SemaphoreType.DMA((6, 20)),
         ],
         compiler_params=pltpu.CompilerParams(
             collective_id=0, has_side_effects=True, vmem_limit_bytes=67043328),

time: 118 us -> 81.2 us (0.69)
  Pallas kernels: 112 us -> 75.5 us
    pallas_call x1, Pallas kernels: 112 us -> 75.5 us  [encode(): pl.pallas_call(functools.partial(kernel, h_count, w_count, rows1), name='...]
where the time goes in v1:
time: 81.2 us; the launch traced here: 80.3 us
  Pallas kernels  75.5 us (93%)
  local copies, waits for them, and re-layouts  4.77 us (6%)
    pallas_call x1, Pallas kernels, encode(): pl.pallas_call(functools.partial(kernel, h_count, w_count, rows1), name='...  75.5 us
    transpose x1, local copies, waits for them, and re-layouts, encode(): return jnp.transpose(out, (2, 0, 1, 3))  3.45 us

profile of v1, /device:TPU:0, one launch (start us, length us, event | category | flops | bytes accessed | tf_op | source)
XLA Modules:
  0.0 80.3 jit_solution(3778309463110403469)
XLA Ops:
  0.0 1.3 %reshape.25.dw1 = bf16[36,32]{1,0:T(8,128)(2,1)} reshape(bf16[3,3,4,32]{3,2,1,0:T(4,128)(2,1)} %param.15) | data formatting | bytes 4608 | tf_op jit(solution)/shard_map/reshape | solution.py:394
  1.3 75.5 %encoder.1 = bf16[32,16,16,128]{3,2,1,0:T(8,128)(2,1)} custom-call(bf16[16,1024,128]{2,1,0:T(8,128)(2,1)} %bitcast.11, bf16[2048,36]{1,0:T(8,128)(2,1)} %constant.2.clone.sel, bf16[36,32]{1,0:T(8,128)(2,1)} %reshape.25.dw1, f32[1,32]{1,0:T(1,128)} %bitcast.12, bf16[3,3,32,32]{3,2,1,0:T(8,128)(2,1)} %rw1.1, f32[1,32]{1,0:T(1,128)} %bitcast.13, ...), custom_call_target="tpu_custom_call" | custom-call | flops 9965666304 | bytes 7340032 | tf_op jit(solution)/shard_map/encoder/pallas_call | solution.py:400
  76.8 3.5 %copy.16 = bf16[16,32,16,128]{3,2,1,0:T(8,128)(2,1)} copy(bf16[16,32,16,128]{3,0,2,1:T(8,128)(2,1)} %bitcast.10) | data formatting | bytes 4194304 | tf_op jit(solution)/shard_map/transpose | solution.py:419

commit v2 on v1

--- a/solution.py
+++ b/solution.py
@@ -12,6 +12,9 @@
 F32 = jnp.float32
 N = 16
 G = 16
+TILES = 4
+DOWN1_ROWS = 16
+PAIRS = 4
 MESH = pl.DeviceIdType.MESH
 
 
@@ -256,7 +259,7 @@
 
 
 def kernel(h_count, w_count, rows1, x_hbm, sel, dw1, db1, rw1, rb1, dw2, db2, rw2, rb2, dw3, db3, rw3, rb3, out,
-           x, pv, y1, z1, y2, z2, y3, bw1, br1, bw2, br2, bw3, br3,
+           x, pv, y1, z1, y2, z2, y3, w36, bw1, br1, bw2, br2, bw3, br3,
            send_x, recv_x, send_c, recv_c, x_sem, send_sem, recv_sem):
     rows2, rows3 = rows1 // 2, rows1 // 4
     me_h, me_w = lax.axis_index('h'), lax.axis_index('w')
@@ -276,7 +279,9 @@
     for dh, dw in others:
         pl.semaphore_signal(barrier, inc=1, device_id=device(dh, dw), device_id_type=MESH)
 
-    picked = jnp.dot(sel[...], dw1[...], preferred_element_type=F32).astype(BF)
+    for k in range(9):
+        w36[4 * k:4 * k + 4, :] = dw1[k].astype(F32)
+    picked = jnp.dot(sel[...], w36[...].astype(BF), preferred_element_type=F32).astype(BF)
     bw1[...] = jnp.concatenate([picked[j * 256:(j + 1) * 256] for j in range(8)], axis=1)
     build_weight(br1, rw1, REFINE1_K, 1)
     build_weight(bw2, dw2, DOWN2_K, 2)
@@ -312,24 +317,25 @@
         return new
 
     def to_pairs(i, carry):
-        t = jnp.transpose(x[:, pl.ds(i * 16, 16), :], (1, 0, 2))
-        for p in range(2):
-            v = [t[p * 8 + k] for k in range(8)]
-            for dist, blocks in ((64, 4), (32, 2), (16, 1)):
-                v = swap(v, dist, blocks)
-            for q in range(8):
-                pv[1 + 2 * i + p, 1 + q] = v[q]
+        for u in range(TILES):
+            t = jnp.transpose(x[:, pl.ds((i * TILES + u) * 16, 16), :], (1, 0, 2))
+            for p in range(2):
+                v = [t[p * 8 + k] for k in range(8)]
+                for dist, blocks in ((64, 4), (32, 2), (16, 1)):
+                    v = swap(v, dist, blocks)
+                for q in range(8):
+                    pv[1 + 2 * (i * TILES + u) + p, 1 + q] = v[q]
         return carry
 
     for i, (lo, hi) in enumerate(image_blocks):
         loads[i].wait()
-        lax.fori_loop(lo // 2, hi // 2, to_pairs, 0)
+        lax.fori_loop(lo // 2 // TILES, hi // 2 // TILES, to_pairs, 0)
         if i == 0:
             pl.semaphore_wait(barrier, len(others))
         pv_halo.send(lo, hi)
 
     bias1 = tiled_bias(db1)
-    per = 8
+    per = DOWN1_ROWS
     size = per * 8 * N
 
     def down1(i, carry):
@@ -349,7 +355,7 @@
                 y1[row0 + 1 + r, 2 + 2 * q] = val[r, q, :, 128:]
         return carry
 
-    for lo, hi in row_blocks(rows1, 8, 32):
+    for lo, hi in row_blocks(rows1, 16, 32):
         pv_halo.need(lo - 1, hi)
         lax.fori_loop(lo // per, hi // per, down1, 0)
         y1_halo.send(lo, hi)
@@ -365,21 +371,21 @@
     def refine(stage, src, src_halo, weight, bias, dst, dst_halo, blocks):
         for lo, hi in blocks:
             src_halo.need(lo - 1, hi + 1)
-            conv_rows(functools.partial(refine_lhs, stage, src), weight, bias, dst, lo, hi, 0, G, 2)
+            conv_rows(functools.partial(refine_lhs, stage, src), weight, bias, dst, lo, hi, 0, G, PAIRS)
             if dst_halo is not None:
                 dst_halo.send(lo, hi)
 
     def down(src, src_halo, weight, bias, dst, dst_halo, blocks):
         for lo, hi in blocks:
             src_halo.need(2 * lo - 1, 2 * hi)
-            conv_rows(functools.partial(down_lhs, src), weight, bias, dst, lo, hi, 0, G, 2)
+            conv_rows(functools.partial(down_lhs, src), weight, bias, dst, lo, hi, 0, G, PAIRS)
             dst_halo.send(lo, hi)
 
-    refine(1, y1, y1_halo, br1, tiled_bias(rb1), into(z1), z1_halo, row_blocks(rows1, 12, 32))
-    down(z1, z1_halo, bw2, tiled_bias(db2), into(y2), y2_halo, row_blocks(rows2, 8, 16))
-    refine(2, y2, y2_halo, br2, tiled_bias(rb2), into(z2), z2_halo, row_blocks(rows2, 12, 16))
-    down(z2, z2_halo, bw3, tiled_bias(db3), into(y3), y3_halo, row_blocks(rows3, 8, 8))
-    refine(3, y3, y3_halo, br3, tiled_bias(rb3), into_out, None, row_blocks(rows3, 12, 8))
+    refine(1, y1, y1_halo, br1, tiled_bias(rb1), into(z1), z1_halo, row_blocks(rows1, 24, 32))
+    down(z1, z1_halo, bw2, tiled_bias(db2), into(y2), y2_halo, row_blocks(rows2, 16, 16))
+    refine(2, y2, y2_halo, br2, tiled_bias(rb2), into(z2), z2_halo, row_blocks(rows2, 24, 16))
+    down(z2, z2_halo, bw3, tiled_bias(db3), into(y3), y3_halo, row_blocks(rows3, 16, 8))
+    refine(3, y3, y3_halo, br3, tiled_bias(rb3), into_out, None, row_blocks(rows3, 24, 8))
 
     for h in (pv_halo, y1_halo, z1_halo, y2_halo, z2_halo, y3_halo):
         h.finish()
@@ -391,7 +397,7 @@
     x = jnp.transpose(images, (0, 1, 3, 2)).reshape(N, rows1 * 8, 128)
     args = [x, jnp.asarray(first_weight_selector(), BF)]
     for i, p in enumerate(params):
-        args.append(p.reshape(1, -1) if i % 2 else (p.reshape(36, 32) if i == 0 else p))
+        args.append(p.reshape(1, -1) if i % 2 else (p.reshape(9, 4, 32) if i == 0 else p))
 
     def act(rows, groups):
         return pltpu.VMEM((rows, groups, N, 128), BF)
@@ -406,14 +412,14 @@
         scratch_shapes=[
             pltpu.VMEM((N, rows1 * 8, 128), BF), act(rows1 + 1, 9), act(rows1 + 2, G + 2), act(rows1 + 1, G + 1),
             act(rows2 + 2, G + 2), act(rows2 + 1, G + 1), act(rows3 + 2, G + 2),
-            pltpu.VMEM((256, 256), BF), pltpu.VMEM((768, 256), BF), pltpu.VMEM((1024, 256), BF),
+            pltpu.VMEM((36, 32), F32), pltpu.VMEM((256, 256), BF), pltpu.VMEM((768, 256), BF), pltpu.VMEM((1024, 256), BF),
             pltpu.VMEM((1024, 256), BF), pltpu.VMEM((1024, 256), BF), pltpu.VMEM((1536, 256), BF),
             pltpu.VMEM((1, rows1 // 16, N, 128), BF), pltpu.VMEM((1, rows1 // 16, N, 128), BF),
             pltpu.VMEM((4, 2, rows1 // 4, N, 128), BF), pltpu.VMEM((4, 2, rows1 // 4, N, 128), BF),
             pltpu.SemaphoreType.DMA((8,)), pltpu.SemaphoreType.DMA((6, 20)), pltpu.SemaphoreType.DMA((6, 20)),
         ],
         compiler_params=pltpu.CompilerParams(
-            collective_id=0, has_side_effects=True, vmem_limit_bytes=67043328),
+            collective_id=0, has_side_effects=True, vmem_limit_bytes=56 * 2**20),
         cost_estimate=pl.CostEstimate(flops=flops, bytes_accessed=7 * 2**20, transcendentals=0),
     )(*args)
     return jnp.transpose(out, (2, 0, 1, 3))

time: 81.2 us -> 66.6 us (0.82)
  Pallas kernels: 75.5 us -> 62.9 us
  local copies, waits for them, and re-layouts: 4.77 us -> 3.45 us
    pallas_call x1, Pallas kernels: 75.5 us -> 62.9 us  [encode(): pl.pallas_call(functools.partial(kernel, h_count, w_count, rows1), name='...]
    reshape x1 -> x0, local copies, waits for them, and re-layouts: 1.31 us -> none  [encode(): p.reshape(36, 32)]
where the time goes in v2:
time: 66.6 us; the launch traced here: 66.4 us
  Pallas kernels  62.9 us (94%)
  local copies, waits for them, and re-layouts  3.45 us (5%)
    pallas_call x1, Pallas kernels, encode(): pl.pallas_call(functools.partial(kernel, h_count, w_count, rows1), name='...  62.9 us
    transpose x1, local copies, waits for them, and re-layouts, encode(): return jnp.transpose(out, (2, 0, 1, 3))  3.45 us

profile of v2, /device:TPU:0, one launch (start us, length us, event | category | flops | bytes accessed | tf_op | source)
XLA Modules:
  0.0 66.4 jit_solution(9091609980193858991)
XLA Ops:
  0.0 62.9 %encoder.1 = bf16[32,16,16,128]{3,2,1,0:T(8,128)(2,1)} custom-call(bf16[16,1024,128]{2,1,0:T(8,128)(2,1)} %bitcast.12, bf16[2048,36]{1,0:T(8,128)(2,1)} %constant.2.clone.sel, bf16[9,4,32]{2,1,0:T(4,128)(2,1)} %bitcast.13, f32[1,32]{1,0:T(1,128)} %bitcast.14, bf16[3,3,32,32]{3,2,1,0:T(8,128)(2,1)} %rw1.1, f32[1,32]{1,0:T(1,128)} %bitcast.15, ...), custom_call_target="tpu_custom_call" | custom-call | flops 9965666304 | bytes 7340032 | tf_op jit(solution)/shard_map/encoder/pallas_call | solution.py:406
  62.9 3.5 %copy.15 = bf16[16,32,16,128]{3,2,1,0:T(8,128)(2,1)} copy(bf16[16,32,16,128]{3,0,2,1:T(8,128)(2,1)} %bitcast.11) | data formatting | bytes 4194304 | tf_op jit(solution)/shard_map/transpose | solution.py:425

commit v3 on v2

v3 whole, which is shorter than its diff:
```python
import functools

import jax
import jax.numpy as jnp
import numpy as np
from jax import lax
from jax.experimental import pallas as pl
from jax.experimental.pallas import tpu as pltpu
from jax.sharding import PartitionSpec as P

BF = jnp.bfloat16
F32 = jnp.float32
N = 16
G = 16
TILES = 4
DOWN1_ROWS = 16
PAIRS = 4
MESH = pl.DeviceIdType.MESH


def first_weight_selector():
    sel = np.zeros((8, 256, 36), np.float32)
    for j in range(8):
        for c in range(4):
            for wi in range(16):
                b = wi - 2 * j + 1
                if 0 <= b <= 2:
                    for hi in range(2):
                        sel[j, hi * 64 + c * 16 + wi, ((hi + 1) * 3 + b) * 4 + c] = 1
                    sel[j, 128 + 64 + c * 16 + wi, (0 * 3 + b) * 4 + c] = 1
            if j == 0:
                for a, wi in ((1, 15), (2, 14), (0, 13)):
                    sel[j, 128 + c * 16 + wi, (a * 3) * 4 + c] = 1
    return sel.reshape(8 * 256, 36)


def roll(v, shift):
    shift %= 128
    return v if shift == 0 else pltpu.roll(v, shift, v.ndim - 1)


def flat(v):
    return v.reshape(-1, 128)


def build_weight(big, w, k_blocks, stride):
    cin, cout = w.shape[2], w.shape[3]
    ncols = 128 // cout
    taps = [[w[a, b] for b in range(3)] for a in range(3)]
    zero = jnp.zeros((cin, cout), BF)
    for kp, pos in enumerate(k_blocks):
        pieces = []
        for orow in range(2):
            for j in range(ncols):
                piece = zero
                if pos is not None:
                    a, b = pos[0] - stride * orow, pos[1] - stride * j + 1
                    if 0 <= a <= 2 and 0 <= b <= 2:
                        piece = taps[a][b]
                pieces.append(piece)
        big[kp * cin:(kp + 1) * cin, :] = jnp.concatenate(pieces, axis=1)


REFINE1_K = ([(ir, ic) for ir in range(4) for ic in range(4)]
             + [p for e in (0, 2) for p in ((e, 4), (e + 1, -1), (e + 1, 4), (e, -1))])
REFINE2_K = ([(ir, ic) for ir in range(4) for ic in range(2)]
             + [p for ir in range(4) for p in ((ir, 2), (ir, -1))])
REFINE3_K = [(ir, ic) for ir in range(4) for ic in (-1, 0, 1)]
DOWN2_K = ([(ir, ic) for ir in range(5) for ic in range(4)]
           + [p for e in (0, 2) for p in (None, (e + 1, -1), None, (e, -1))]
           + [None, None, None, (4, -1)])
DOWN3_K = ([(ir, ic) for ir in range(5) for ic in range(2)]
           + [p for e in (0, 2) for p in ((e + 1, -1), (e, -1))] + [None, (4, -1)])


def tiled_bias(b):
    reps = 128 // b.shape[1]
    return jnp.concatenate([b[...]] * (2 * reps), axis=1)


def refine_lhs(stage, src, p0, pairs, g0, ng):
    def rows(h, g):
        return flat(src[pl.ds(p0 + (h + 1) // 2, pairs), (h + 1) % 2, pl.ds(g, ng)])

    def own(h):
        return rows(h, 1 + g0)

    def left(h):
        return rows(h, g0)

    def right(h):
        return rows(h, 2 + g0)

    def edge(h):
        return jnp.concatenate([right(h)[:, :64], left(h)[:, 64:]], axis=1)

    if stage == 3:
        return [f(h) for h in range(4) for f in (left, own, right)]
    if stage == 2:
        return [own(h) for h in range(4)] + [edge(h) for h in range(4)]
    ks = [own(h) for h in range(4)]
    for h in (0, 2):
        f0, f1 = edge(h), roll(edge(h + 1), 64)
        ks.append(jnp.concatenate([f0[:, :32], f1[:, 32:96], f0[:, 96:]], axis=1))
    return ks


def down_lhs(src, p0, pairs, g0, ng):
    def rows(h, g):
        return flat(src[pl.ds(p0 + (h + 3) // 4, pairs), (h + 3) % 4, pl.ds(g, ng)])

    def own(h):
        return rows(h, 1 + g0)

    def left(h):
        return rows(h, g0)

    ks = [own(h) for h in range(5)]
    for h in (0, 2):
        ks.append(jnp.concatenate([roll(left(h + 1), 64)[:, :64], left(h)[:, 64:]], axis=1))
    return ks + [left(4)]


def conv_rows(lhs, weight, bias, dst, lo, hi, ranges, pairs):
    pairs = min(pairs, (hi - lo) // 2)

    def step(i, carry):
        p0 = lo // 2 + i * pairs
        parts = [lhs(p0, pairs, g0, ng) for g0, ng in ranges]
        ks = [jnp.concatenate(part, axis=0) if len(ranges) > 1 else part[0] for part in zip(*parts)]
        res = jnp.dot(jnp.concatenate(ks, axis=1), weight[...], preferred_element_type=F32)
        val = jnp.maximum(res + bias, 0.0).astype(BF)
        at = 0
        for g0, ng in ranges:
            size = pairs * ng * N
            tile = val[at:at + size]
            at += size
            dst(lo // 4 + i * (pairs // 2), p0, pairs, g0, ng, tile)
        return carry

    lax.fori_loop(0, (hi - lo) // (2 * pairs), step, 0)


def into_pairs(buf, shift):
    def dst(quad0, p0, pairs, g0, ng, tile):
        for half in range(2):
            buf[pl.ds(p0 + shift, pairs), half, pl.ds(g0 + shift, ng)] = (
                tile[:, half * 128:(half + 1) * 128].reshape(pairs, ng, N, 128))
    return dst


def into_quads(buf):
    def dst(quad0, p0, pairs, g0, ng, tile):
        for half in range(2):
            v = tile[:, half * 128:(half + 1) * 128].reshape(pairs // 2, 2, ng, N, 128)
            for odd in range(2):
                buf[pl.ds(quad0 + 1, pairs // 2), 2 * odd + half, pl.ds(1 + g0, ng)] = v[:, odd]
    return dst


def pack_cols(stage, buf, lo, hi, right_edge):
    view = buf.shape[1]
    col = buf[pl.ds(lo // view + 1, (hi - lo) // view), :, G if right_edge else 1]
    per = 4 if stage == 1 else 2
    width = 128 // per
    col = col.reshape((hi - lo) // per, per, N, 128)
    base = 128 - width if right_edge else 0
    parts = []
    for k in range(per):
        v = roll(flat(col[:, k]), k * width - base)
        parts.append(v[:, k * width:(k + 1) * width])
    return jnp.concatenate(parts, axis=1).reshape((hi - lo) // per, N, 128)


def unpack_cols(stage, buf, lo, hi, packed, left_halo):
    view = buf.shape[1]
    per = 4 if stage == 1 else 2
    width = 128 // per
    base = 128 - width if left_halo else 0
    tiles = flat(packed)
    rows = [roll(tiles, base - k * width).reshape(-1, N, 128) for k in range(per)]
    buf[pl.ds(lo // view + 1, (hi - lo) // view), :, 0 if left_halo else G + 1] = (
        jnp.stack(rows, axis=1).reshape((hi - lo) // view, view, N, 128))


def pack_image(pv, lo, hi):
    rows = hi - lo
    col = pv[pl.ds(1 + lo, rows), 8].reshape(rows // 16, 16, N, 128)
    lanes = lax.broadcasted_iota(jnp.int16, (rows, 128), 1) & 15
    packed = flat(col[:, 15])
    for k in range(15):
        packed = jnp.where(lanes == k, roll(flat(col[:, k]), k - 15), packed)
    return packed.reshape(rows // 16, N, 128)


def unpack_image(pv, lo, hi, packed):
    tiles = flat(packed)
    rows = [roll(tiles, 15 - k).reshape(-1, N, 128) for k in range(16)]
    pv[pl.ds(1 + lo, hi - lo), 0] = jnp.stack(rows, axis=1).reshape(hi - lo, N, 128)


def row_blocks(rows, start, size):
    out = [(lo, min(lo + size, rows)) for lo in range(start, rows, size)]
    return out + [(lo, min(lo + size, start)) for lo in range(0, start, size)]


class Halo:
    def __init__(self, stage, buf, rows, groups, both, send_c, recv_c, sems, device):
        self.stage, self.buf, self.rows, self.groups, self.both = stage, buf, rows, groups, both
        self.send_c, self.recv_c, self.sems, self.device = send_c, recv_c, sems, device
        self.count, self.sent, self.chunks = 0, [], []
        self.slabs, self.corners = {'top': [], 'bottom': []}, {'top': [], 'bottom': []}

    def copy(self, src, dst, direction):
        send_sem, recv_sem = self.sems
        c = pltpu.make_async_remote_copy(
            src_ref=src, dst_ref=dst, send_sem=send_sem.at[self.count], recv_sem=recv_sem.at[self.count],
            device_id=self.device(*direction), device_id_type=MESH)
        self.count += 1
        self.sent.append(c)
        c.start()
        return c

    def send_cols(self, lo, hi, side):
        buf, stage = self.buf, self.stage
        if stage == 3:
            part = pl.ds(lo // 2 + 1, (hi - lo) // 2)
            src = buf.at[part, :, G if side == 0 else 1]
            dst = buf.at[part, :, 0 if side == 0 else G + 1]
        else:
            per = {0: 16, 1: 4, 2: 2}[stage]
            part = pl.ds(lo // per, (hi - lo) // per)
            self.send_c[side, part] = (
                pack_image(buf, lo, hi) if stage == 0 else pack_cols(stage, buf, lo, hi, side == 0))
            src, dst = self.send_c.at[side, part], self.recv_c.at[side, part]
        self.chunks.append((lo, hi, side, self.copy(src, dst, (0, 1 if side == 0 else -1))))

    def cells(self, row, groups):
        view = self.buf.shape[1] if self.stage else 1
        at = (row // view + 1, row % view) if self.stage else (row + 1,)
        return self.buf.at[at + (groups,)]

    def send_rows(self, lo, hi):
        last, ng, cells = self.rows - 1, self.groups, self.cells
        every = pl.ds(1, ng)
        if hi == self.rows:
            self.slabs['top'].append(self.copy(cells(last, every), cells(-1, every), (1, 0)))
            self.corners['top'].append(self.copy(cells(last, ng), cells(-1, 0), (1, 1)))
            if self.both:
                self.corners['top'].append(self.copy(cells(last, 1), cells(-1, ng + 1), (1, -1)))
        if lo == 0 and self.both:
            self.slabs['bottom'].append(self.copy(cells(0, every), cells(last + 1, every), (-1, 0)))
            self.corners['bottom'].append(self.copy(cells(0, ng), cells(last + 1, 0), (-1, 1)))
            self.corners['bottom'].append(self.copy(cells(0, 1), cells(last + 1, ng + 1), (-1, -1)))

    def ends(self, which, lo, hi):
        for end, wanted in (('top', lo < 0), ('bottom', hi > self.rows)):
            if wanted:
                for c in which[end]:
                    c.wait_recv()
                which[end] = []

    def need_rows(self, lo, hi):
        self.ends(self.slabs, lo, hi)

    def need_cols(self, lo, hi):
        left = []
        for chunk in self.chunks:
            first, end, side, c = chunk
            if first < hi and lo < end:
                c.wait_recv()
                if self.stage != 3:
                    per = {0: 16, 1: 4, 2: 2}[self.stage]
                    packed = self.recv_c[side, pl.ds(first // per, (end - first) // per)]
                    if self.stage == 0:
                        unpack_image(self.buf, first, end, packed)
                    else:
                        unpack_cols(self.stage, self.buf, first, end, packed, side == 0)
            else:
                left.append(chunk)
        self.chunks = left
        self.ends(self.corners, lo, hi)

    def finish(self):
        assert not self.chunks and not any(self.slabs.values()) and not any(self.corners.values())
        for c in self.sent:
            c.wait_send()


def schedule(blocks, delay):
    out = []
    for i in range(len(blocks) + delay):
        if i < len(blocks):
            out.append((False, blocks[i]))
        if i >= delay and i - delay < len(blocks):
            out.append((True, blocks[i - delay]))
    return out


def kernel(h_count, w_count, rows1, x_hbm, sel, dw1, db1, rw1, rb1, dw2, db2, rw2, rb2, dw3, db3, rw3, rb3, out,
           x, pv, y1, z1, y2, z2, y3, w36, bw1, br1, bw2, br2, bw3, br3,
           send_x, recv_x, send_c, recv_c, x_sem, send_sem, recv_sem):
    rows2, rows3 = rows1 // 2, rows1 // 4
    me_h, me_w = lax.axis_index('h'), lax.axis_index('w')

    image_blocks = row_blocks(rows1, 0, 32)
    loads = []
    for i, (lo, hi) in enumerate(image_blocks):
        part = pl.ds(lo * 8, (hi - lo) * 8)
        loads.append(pltpu.make_async_copy(x_hbm.at[:, part], x.at[:, part], x_sem.at[i]))
        loads[-1].start()

    def device(dh, dw):
        return {'h': lax.rem(me_h + dh + h_count, h_count), 'w': lax.rem(me_w + dw + w_count, w_count)}

    barrier = pltpu.get_barrier_semaphore()
    others = [(dh, dw) for dh in (-1, 0, 1) for dw in (-1, 0, 1) if dh or dw]
    for dh, dw in others:
        pl.semaphore_signal(barrier, inc=1, device_id=device(dh, dw), device_id_type=MESH)

    for k in range(9):
        w36[4 * k:4 * k + 4, :] = dw1[k].astype(F32)
    picked = jnp.dot(sel[...], w36[...].astype(BF), preferred_element_type=F32).astype(BF)
    bw1[...] = jnp.concatenate([picked[j * 256:(j + 1) * 256] for j in range(8)], axis=1)
    build_weight(br1, rw1, REFINE1_K, 1)
    build_weight(bw2, dw2, DOWN2_K, 2)
    build_weight(br2, rw2, REFINE2_K, 1)
    build_weight(bw3, dw3, DOWN3_K, 2)
    build_weight(br3, rw3, REFINE3_K, 1)

    def halo(e, stage, buf, rows, groups, both):
        sems = (send_sem.at[e], recv_sem.at[e])
        if stage == 0:
            return Halo(stage, buf, rows, groups, both, send_x, recv_x, sems, device)
        if stage == 3:
            return Halo(stage, buf, rows, groups, both, None, None, sems, device)
        return Halo(stage, buf, rows, groups, both, send_c.at[e - 1], recv_c.at[e - 1], sems, device)

    pv_halo = halo(0, 0, pv, rows1, 8, False)
    y1_halo = halo(1, 1, y1, rows1, G, True)
    z1_halo = halo(2, 1, z1, rows1, G, False)
    y2_halo = halo(3, 2, y2, rows2, G, True)
    z2_halo = halo(4, 2, z2, rows2, G, False)
    y3_halo = halo(5, 3, y3, rows3, G, True)

    lane = lax.broadcasted_iota(jnp.int16, (N, 128), 1)

    def swap(v, dist, blocks):
        mask = (lane & dist) == 0
        new = list(v)
        for i in range(8):
            if not i & blocks:
                a, b = v[i], v[i + blocks]
                new[i] = jnp.where(mask, a, roll(b, dist))
                new[i + blocks] = jnp.where(mask, roll(a, -dist), b)
        return new

    def to_pairs(i, carry):
        for u in range(TILES):
            t = jnp.transpose(x[:, pl.ds((i * TILES + u) * 16, 16), :], (1, 0, 2))
            for p in range(2):
                v = [t[p * 8 + k] for k in range(8)]
                for dist, blocks in ((64, 4), (32, 2), (16, 1)):
                    v = swap(v, dist, blocks)
                pv[1 + 2 * (i * TILES + u) + p, pl.ds(1, 8)] = jnp.stack(v)
        return carry

    for i, (lo, hi) in enumerate(image_blocks):
        loads[i].wait()
        lax.fori_loop(lo // 2 // TILES, hi // 2 // TILES, to_pairs, 0)
        if i == 0:
            pl.semaphore_wait(barrier, len(others))
        pv_halo.send_cols(lo, hi, 0)
        pv_halo.send_rows(lo, hi)

    bias1 = tiled_bias(db1)

    def down1(lo, hi, q0, nq, per):
        per = min(per, hi - lo)
        size = per * nq * N

        def step(i, carry):
            row0 = lo + i * per
            sub = lax.broadcasted_iota(jnp.int16, (size, 128), 1) & 15
            own = flat(pv[pl.ds(row0 + 1, per), pl.ds(1 + q0, nq)])
            above = flat(pv[pl.ds(row0, per), pl.ds(1 + q0, nq)])
            left = flat(pv[pl.ds(row0 + 1, per), pl.ds(q0, nq)])
            above_left = flat(pv[pl.ds(row0, per), pl.ds(q0, nq)])
            edge = jnp.where(sub == 15, left, jnp.where(sub == 14, roll(left, 63), roll(above_left, 62)))
            second = jnp.concatenate([edge[:, :64], above[:, 64:]], axis=1)
            res = jnp.dot(jnp.concatenate([own, second], axis=1), bw1[...], preferred_element_type=F32)
            val = jnp.maximum(res + bias1, 0.0).astype(BF)
            pairs = pl.ds(lo // 2 + i * (per // 2) + 1, per // 2)
            for half in range(2):
                v = val[:, half * 128:(half + 1) * 128].reshape(per // 2, 2, nq, N, 128)
                for q in range(nq):
                    y1[pairs, :, 1 + 2 * (q0 + q) + half] = v[:, :, q]
            return carry

        lax.fori_loop(0, (hi - lo) // per, step, 0)

    for is_edge, (lo, hi) in schedule(row_blocks(rows1, 16, 32), 1):
        if is_edge:
            pv_halo.need_cols(lo - 1, hi)
            down1(lo, hi, 0, 1, 32)
            y1_halo.send_cols(lo, hi, 1)
            y1_halo.send_rows(lo, hi)
        else:
            pv_halo.need_rows(lo - 1, hi)
            down1(lo, hi, 1, 7, DOWN1_ROWS)
            y1_halo.send_cols(lo, hi, 0)

    def refine(stage, src, src_halo, weight, bias, dst, dst_halo, blocks, delay):
        lhs = functools.partial(refine_lhs, stage, src)
        for is_edge, (lo, hi) in schedule(blocks, delay):
            if is_edge:
                src_halo.need_cols(lo - 1, hi + 1)
                conv_rows(lhs, weight, bias, dst, lo, hi, [(0, 1), (G - 1, 1)], 16)
                if dst_halo is not None:
                    dst_halo.send_cols(lo, hi, 0)
                    dst_halo.send_rows(lo, hi)
            else:
                src_halo.need_rows(lo - 1, hi + 1)
                conv_rows(lhs, weight, bias, dst, lo, hi, [(1, G - 2)], PAIRS)

    def down(src, src_halo, weight, bias, dst, dst_halo, blocks, delay):
        lhs = functools.partial(down_lhs, src)
        for is_edge, (lo, hi) in schedule(blocks, delay):
            if is_edge:
                src_halo.need_cols(2 * lo - 1, 2 * hi)
                conv_rows(lhs, weight, bias, dst, lo, hi, [(0, 1)], 16)
                dst_halo.send_cols(lo, hi, 1)
                dst_halo.send_rows(lo, hi)
            else:
                src_halo.need_rows(2 * lo - 1, 2 * hi)
                conv_rows(lhs, weight, bias, dst, lo, hi, [(1, G - 1)], PAIRS)
                dst_halo.send_cols(lo, hi, 0)

    refine(1, y1, y1_halo, br1, tiled_bias(rb1), into_quads(z1), z1_halo, row_blocks(rows1, 24, 32), 1)
    down(z1, z1_halo, bw2, tiled_bias(db2), into_pairs(y2, 1), y2_halo, row_blocks(rows2, 16, 16), 1)
    refine(2, y2, y2_halo, br2, tiled_bias(rb2), into_quads(z2), z2_halo, row_blocks(rows2, 24, 16), 1)
    down(z2, z2_halo, bw3, tiled_bias(db3), into_pairs(y3, 1), y3_halo, row_blocks(rows3, 16, 8), 4)
    refine(3, y3, y3_halo, br3, tiled_bias(rb3), into_pairs(out, 0), None,
           [(4, rows3 - 4), (rows3 - 4, rows3), (0, 4)], 3)

    for h in (pv_halo, y1_halo, z1_halo, y2_halo, z2_halo, y3_halo):
        h.finish()


def encode(h_count, w_count, images, *params):
    rows1 = images.shape[1] // 2
    rows2, rows3 = rows1 // 2, rows1 // 4
    x = jnp.transpose(images, (0, 1, 3, 2)).reshape(N, rows1 * 8, 128)
    args = [x, jnp.asarray(first_weight_selector(), BF)]
    for i, p in enumerate(params):
        args.append(p.reshape(1, -1) if i % 2 else (p.reshape(9, 4, 32) if i == 0 else p))

    def act(*shape):
        return pltpu.VMEM(shape + (N, 128), BF)

    flops = 2 * 16 * rows1 * 64 * 32 * 9 * (4 + 32 + 16 + 32 + 16 + 32)
    out = pl.pallas_call(
        functools.partial(kernel, h_count, w_count, rows1),
        name='encoder',
        out_shape=jax.ShapeDtypeStruct((rows3 // 2, 2, G, N, 128), BF),
        in_specs=[pl.BlockSpec(memory_space=pl.ANY)] + [pl.BlockSpec(memory_space=pltpu.VMEM)] * (len(args) - 1),
        out_specs=pl.BlockSpec(memory_space=pltpu.VMEM),
        scratch_shapes=[
            pltpu.VMEM((N, rows1 * 8, 128), BF), act(rows1 + 1, 9),
            act(rows1 // 2 + 2, 2, G + 2), act(rows1 // 4 + 1, 4, G + 1),
            act(rows2 // 2 + 2, 2, G + 2), act(rows2 // 4 + 1, 4, G + 1), act(rows3 // 2 + 2, 2, G + 2),
            pltpu.VMEM((36, 32), F32), pltpu.VMEM((256, 256), BF), pltpu.VMEM((768, 256), BF), pltpu.VMEM((1024, 256), BF),
            pltpu.VMEM((1024, 256), BF), pltpu.VMEM((1024, 256), BF), pltpu.VMEM((1536, 256), BF),
            pltpu.VMEM((1, rows1 // 16, N, 128), BF), pltpu.VMEM((1, rows1 // 16, N, 128), BF),
            pltpu.VMEM((4, 2, rows1 // 4, N, 128), BF), pltpu.VMEM((4, 2, rows1 // 4, N, 128), BF),
            pltpu.SemaphoreType.DMA((8,)), pltpu.SemaphoreType.DMA((6, 20)), pltpu.SemaphoreType.DMA((6, 20)),
        ],
        compiler_params=pltpu.CompilerParams(
            collective_id=0, has_side_effects=True, vmem_limit_bytes=56 * 2**20),
        cost_estimate=pl.CostEstimate(flops=flops, bytes_accessed=7 * 2**20, transcendentals=0),
    )(*args)
    return jnp.transpose(out.reshape(rows3, G, N, 128), (2, 0, 1, 3))


def solution(mesh):
    tile_spec = P('batch', 'h', 'w', None)
    body = functools.partial(encode, mesh.shape['h'], mesh.shape['w'])
    return jax.shard_map(body, mesh=mesh, in_specs=(tile_spec,) + (P(),) * 12, out_specs=tile_spec, check_vma=False)
```

time: 66.6 us -> 67.6 us (1.015)
  Pallas kernels: 62.9 us -> 64 us
    reshape x0 -> x1, local copies, waits for them, and re-layouts: none -> 3.45 us  [encode(): return jnp.transpose(out.reshape(rows3, G, N, 128), (2, 0, 1, 3))]
    transpose x1 -> x0, local copies, waits for them, and re-layouts: 3.45 us -> none  [encode(): return jnp.transpose(out, (2, 0, 1, 3))]
    pallas_call x1, Pallas kernels: 62.9 us -> 64 us  [encode(): pl.pallas_call(functools.partial(kernel, h_count, w_count, rows1), name='...]
where the time goes in v3:
time: 67.6 us; the launch traced here: 67.5 us
  Pallas kernels  64 us (95%)
  local copies, waits for them, and re-layouts  3.45 us (5%)
    pallas_call x1, Pallas kernels, encode(): pl.pallas_call(functools.partial(kernel, h_count, w_count, rows1), name='...  64 us
    reshape x1, local copies, waits for them, and re-layouts, encode(): return jnp.transpose(out.reshape(rows3, G, N, 128), (2, 0, 1, 3))  3.45 us

profile of v3, /device:TPU:0, one launch (start us, length us, event | category | flops | bytes accessed | tf_op | source)
XLA Modules:
  0.0 67.5 jit_solution(6695772746671563307)
XLA Ops:
  0.0 64.0 %encoder.1 = bf16[16,2,16,16,128]{4,3,2,1,0:T(8,128)(2,1)} custom-call(bf16[16,1024,128]{2,1,0:T(8,128)(2,1)} %bitcast.15, bf16[2048,36]{1,0:T(8,128)(2,1)} %constant.2.clone.sel, bf16[9,4,32]{2,1,0:T(4,128)(2,1)} %bitcast.16, f32[1,32]{1,0:T(1,128)} %bitcast.17, bf16[3,3,32,32]{3,2,1,0:T(8,128)(2,1)} %rw1.1, f32[1,32]{1,0:T(1,128)} %bitcast.18, ...), custom_call_target="tpu_custom_call" | custom-call | flops 9965666304 | bytes 7340032 | tf_op jit(solution)/shard_map/encoder/pallas_call | solution.py:462
  64.0 3.5 %copy.17 = bf16[32,16,16,128]{3,1,0,2:T(8,128)(2,1)} copy(bf16[32,16,16,128]{3,2,1,0:T(8,128)(2,1)} %bitcast.14) | data formatting | bytes 4194304 | tf_op jit(solution)/shard_map/reshape | solution.py:482

commit v4 on v3

--- a/solution.py
+++ b/solution.py
@@ -13,8 +13,9 @@
 N = 16
 G = 16
 TILES = 4
-DOWN1_ROWS = 16
+DOWN1_ROWS = 8
 PAIRS = 4
+UNROLL = 0
 MESH = pl.DeviceIdType.MESH
 
 
@@ -121,6 +122,24 @@
     return ks + [left(4)]
 
 
+def unrolled(count, step):
+    trips = count // UNROLL if UNROLL else 1
+    each = UNROLL or count
+    if trips <= 1:
+        for i in range(count):
+            step(i, 0)
+        return
+
+    def trip(t, carry):
+        for u in range(each):
+            step(t * each + u, 0)
+        return carry
+
+    lax.fori_loop(0, trips, trip, 0)
+    for i in range(trips * each, count):
+        step(i, 0)
+
+
 def conv_rows(lhs, weight, bias, dst, lo, hi, ranges, pairs):
     pairs = min(pairs, (hi - lo) // 2)
 
@@ -138,7 +157,7 @@
             dst(lo // 4 + i * (pairs // 2), p0, pairs, g0, ng, tile)
         return carry
 
-    lax.fori_loop(0, (hi - lo) // (2 * pairs), step, 0)
+    unrolled((hi - lo) // (2 * pairs), step)
 
 
 def into_pairs(buf, shift):
@@ -397,7 +416,7 @@
                     y1[pairs, :, 1 + 2 * (q0 + q) + half] = v[:, :, q]
             return carry
 
-        lax.fori_loop(0, (hi - lo) // per, step, 0)
+        unrolled((hi - lo) // per, step)
 
     for is_edge, (lo, hi) in schedule(row_blocks(rows1, 16, 32), 1):
         if is_edge:

time: 67.6 us -> 64.9 us (0.960)
  Pallas kernels: 64 us -> 61.2 us
    pallas_call x1, Pallas kernels: 64 us -> 61.2 us  [encode(): pl.pallas_call(functools.partial(kernel, h_count, w_count, rows1), name='...]
where the time goes in v4:
time: 64.9 us; the launch traced here: 64.7 us
  Pallas kernels  61.2 us (94%)
  local copies, waits for them, and re-layouts  3.45 us (5%)
    pallas_call x1, Pallas kernels, encode(): pl.pallas_call(functools.partial(kernel, h_count, w_count, rows1), name='...  61.2 us
    reshape x1, local copies, waits for them, and re-layouts, encode(): return jnp.transpose(out.reshape(rows3, G, N, 128), (2, 0, 1, 3))  3.45 us

profile of v4, /device:TPU:0, one launch (start us, length us, event | category | flops | bytes accessed | tf_op | source)
XLA Modules:
  0.0 64.7 jit_solution(14461741741426612720)
XLA Ops:
  0.0 61.2 %encoder.1 = bf16[16,2,16,16,128]{4,3,2,1,0:T(8,128)(2,1)} custom-call(bf16[16,1024,128]{2,1,0:T(8,128)(2,1)} %bitcast.15, bf16[2048,36]{1,0:T(8,128)(2,1)} %constant.2.clone.sel, bf16[9,4,32]{2,1,0:T(4,128)(2,1)} %bitcast.16, f32[1,32]{1,0:T(1,128)} %bitcast.17, bf16[3,3,32,32]{3,2,1,0:T(8,128)(2,1)} %rw1.1, f32[1,32]{1,0:T(1,128)} %bitcast.18, ...), custom_call_target="tpu_custom_call" | custom-call | flops 9965666304 | bytes 7340032 | tf_op jit(solution)/shard_map/encoder/pallas_call | solution.py:481
  61.3 3.5 %copy.17 = bf16[32,16,16,128]{3,1,0,2:T(8,128)(2,1)} copy(bf16[32,16,16,128]{3,2,1,0:T(8,128)(2,1)} %bitcast.14) | data formatting | bytes 4194304 | tf_op jit(solution)/shard_map/reshape | solution.py:501

commit v5 on v4

--- a/solution.py
+++ b/solution.py
@@ -122,6 +122,10 @@
     return ks + [left(4)]
 
 
+def divisor(count, most):
+    return next(d for d in range(min(most, count), 0, -1) if count % d == 0 and d % 2 == 0)
+
+
 def unrolled(count, step):
     trips = count // UNROLL if UNROLL else 1
     each = UNROLL or count
@@ -141,7 +145,7 @@
 
 
 def conv_rows(lhs, weight, bias, dst, lo, hi, ranges, pairs):
-    pairs = min(pairs, (hi - lo) // 2)
+    pairs = divisor((hi - lo) // 2, pairs)
 
     def step(i, carry):
         p0 = lo // 2 + i * pairs
@@ -387,15 +391,16 @@
     for i, (lo, hi) in enumerate(image_blocks):
         loads[i].wait()
         lax.fori_loop(lo // 2 // TILES, hi // 2 // TILES, to_pairs, 0)
-        if i == 0:
+        if i == 1:
             pl.semaphore_wait(barrier, len(others))
-        pv_halo.send_cols(lo, hi, 0)
+        if i % 2:
+            pv_halo.send_cols(image_blocks[i - 1][0], hi, 0)
         pv_halo.send_rows(lo, hi)
 
     bias1 = tiled_bias(db1)
 
     def down1(lo, hi, q0, nq, per):
-        per = min(per, hi - lo)
+        per = divisor(hi - lo, per)
         size = per * nq * N
 
         def step(i, carry):
@@ -418,7 +423,7 @@
 
         unrolled((hi - lo) // per, step)
 
-    for is_edge, (lo, hi) in schedule(row_blocks(rows1, 16, 32), 1):
+    for is_edge, (lo, hi) in schedule(row_blocks(rows1, 16, 56), 1):
         if is_edge:
             pv_halo.need_cols(lo - 1, hi)
             down1(lo, hi, 0, 1, 32)
@@ -455,10 +460,10 @@
                 conv_rows(lhs, weight, bias, dst, lo, hi, [(1, G - 1)], PAIRS)
                 dst_halo.send_cols(lo, hi, 0)
 
-    refine(1, y1, y1_halo, br1, tiled_bias(rb1), into_quads(z1), z1_halo, row_blocks(rows1, 24, 32), 1)
-    down(z1, z1_halo, bw2, tiled_bias(db2), into_pairs(y2, 1), y2_halo, row_blocks(rows2, 16, 16), 1)
-    refine(2, y2, y2_halo, br2, tiled_bias(rb2), into_quads(z2), z2_halo, row_blocks(rows2, 24, 16), 1)
-    down(z2, z2_halo, bw3, tiled_bias(db3), into_pairs(y3, 1), y3_halo, row_blocks(rows3, 16, 8), 4)
+    refine(1, y1, y1_halo, br1, tiled_bias(rb1), into_quads(z1), z1_halo, row_blocks(rows1, 24, 56), 1)
+    down(z1, z1_halo, bw2, tiled_bias(db2), into_pairs(y2, 1), y2_halo, row_blocks(rows2, 16, 24), 1)
+    refine(2, y2, y2_halo, br2, tiled_bias(rb2), into_quads(z2), z2_halo, row_blocks(rows2, 24, 24), 1)
+    down(z2, z2_halo, bw3, tiled_bias(db3), into_pairs(y3, 1), y3_halo, row_blocks(rows3, 16, 16), 4)
     refine(3, y3, y3_halo, br3, tiled_bias(rb3), into_pairs(out, 0), None,
            [(4, rows3 - 4), (rows3 - 4, rows3), (0, 4)], 3)
 

time: 64.9 us -> 63.2 us (0.974)
  Pallas kernels: 61.2 us -> 59.6 us
    pallas_call x1, Pallas kernels: 61.2 us -> 59.6 us  [encode(): pl.pallas_call(functools.partial(kernel, h_count, w_count, rows1), name='...]
where the time goes in v5:
time: 63.2 us; the launch traced here: 63 us
  Pallas kernels  59.6 us (94%)
  local copies, waits for them, and re-layouts  3.45 us (5%)
    pallas_call x1, Pallas kernels, encode(): pl.pallas_call(functools.partial(kernel, h_count, w_count, rows1), name='...  59.6 us
    reshape x1, local copies, waits for them, and re-layouts, encode(): return jnp.transpose(out.reshape(rows3, G, N, 128), (2, 0, 1, 3))  3.45 us

profile of v5, /device:TPU:0, one launch (start us, length us, event | category | flops | bytes accessed | tf_op | source)
XLA Modules:
  0.0 63.0 jit_solution(1102944744519497198)
XLA Ops:
  0.0 59.6 %encoder.1 = bf16[16,2,16,16,128]{4,3,2,1,0:T(8,128)(2,1)} custom-call(bf16[16,1024,128]{2,1,0:T(8,128)(2,1)} %bitcast.15, bf16[2048,36]{1,0:T(8,128)(2,1)} %constant.2.clone.sel, bf16[9,4,32]{2,1,0:T(4,128)(2,1)} %bitcast.16, f32[1,32]{1,0:T(1,128)} %bitcast.17, bf16[3,3,32,32]{3,2,1,0:T(8,128)(2,1)} %rw1.1, f32[1,32]{1,0:T(1,128)} %bitcast.18, ...), custom_call_target="tpu_custom_call" | custom-call | flops 9965666304 | bytes 7340032 | tf_op jit(solution)/shard_map/encoder/pallas_call | solution.py:486
  59.6 3.5 %copy.17 = bf16[32,16,16,128]{3,1,0,2:T(8,128)(2,1)} copy(bf16[32,16,16,128]{3,2,1,0:T(8,128)(2,1)} %bitcast.14) | data formatting | bytes 4194304 | tf_op jit(solution)/shard_map/reshape | solution.py:506

commit v6 on v5

--- a/solution.py
+++ b/solution.py
@@ -368,23 +368,18 @@
 
     lane = lax.broadcasted_iota(jnp.int16, (N, 128), 1)
 
-    def swap(v, dist, blocks):
-        mask = (lane & dist) == 0
-        new = list(v)
-        for i in range(8):
-            if not i & blocks:
-                a, b = v[i], v[i + blocks]
-                new[i] = jnp.where(mask, a, roll(b, dist))
-                new[i + blocks] = jnp.where(mask, roll(a, -dist), b)
-        return new
+    def to_groups(v):
+        v = [roll(t, 16 * i) for i, t in enumerate(v)]
+        for k in range(3):
+            mask = (lane & (16 << k)) == 0
+            v = [jnp.where(mask, v[j], v[(j + (1 << k)) % 8]) for j in range(8)]
+        return [roll(v[-q % 8], -16 * q) for q in range(8)]
 
     def to_pairs(i, carry):
         for u in range(TILES):
             t = jnp.transpose(x[:, pl.ds((i * TILES + u) * 16, 16), :], (1, 0, 2))
             for p in range(2):
-                v = [t[p * 8 + k] for k in range(8)]
-                for dist, blocks in ((64, 4), (32, 2), (16, 1)):
-                    v = swap(v, dist, blocks)
+                v = to_groups([t[p * 8 + k] for k in range(8)])
                 pv[1 + 2 * (i * TILES + u) + p, pl.ds(1, 8)] = jnp.stack(v)
         return carry
 
@@ -486,13 +481,13 @@
     out = pl.pallas_call(
         functools.partial(kernel, h_count, w_count, rows1),
         name='encoder',
-        out_shape=jax.ShapeDtypeStruct((rows3 // 2, 2, G, N, 128), BF),
+        out_shape=pltpu.VMEM((rows3 // 2, 2, G, N, 128), BF),
         in_specs=[pl.BlockSpec(memory_space=pl.ANY)] + [pl.BlockSpec(memory_space=pltpu.VMEM)] * (len(args) - 1),
         out_specs=pl.BlockSpec(memory_space=pltpu.VMEM),
         scratch_shapes=[
-            pltpu.VMEM((N, rows1 * 8, 128), BF), act(rows1 + 1, 9),
-            act(rows1 // 2 + 2, 2, G + 2), act(rows1 // 4 + 1, 4, G + 1),
-            act(rows2 // 2 + 2, 2, G + 2), act(rows2 // 4 + 1, 4, G + 1), act(rows3 // 2 + 2, 2, G + 2),
+            pltpu.VMEM((N, rows1 * 8 + 16, 128), BF), act(rows1 + 1, 9),
+            act(rows1 // 2 + 2, 2, G + 3), act(rows1 // 4 + 1, 4, G + 1),
+            act(rows2 // 2 + 2, 2, G + 3), act(rows2 // 4 + 1, 4, G + 1), act(rows3 // 2 + 2, 2, G + 3),
             pltpu.VMEM((36, 32), F32), pltpu.VMEM((256, 256), BF), pltpu.VMEM((768, 256), BF), pltpu.VMEM((1024, 256), BF),
             pltpu.VMEM((1024, 256), BF), pltpu.VMEM((1024, 256), BF), pltpu.VMEM((1536, 256), BF),
             pltpu.VMEM((1, rows1 // 16, N, 128), BF), pltpu.VMEM((1, rows1 // 16, N, 128), BF),

time: 63.2 us -> 57.7 us (0.913)
  Pallas kernels: 59.6 us -> 55.7 us
  local copies, waits for them, and re-layouts: 3.45 us -> 1.86 us
    pallas_call x1, Pallas kernels: 59.6 us -> 55.7 us  [encode(): pl.pallas_call(functools.partial(kernel, h_count, w_count, rows1), name='...]
    reshape x1, local copies, waits for them, and re-layouts: 3.45 us -> 1.86 us  [encode(): return jnp.transpose(out.reshape(rows3, G, N, 128), (2, 0, 1, 3))]
where the time goes in v6:
time: 57.7 us; the launch traced here: 57.5 us
  Pallas kernels  55.7 us (97%)
  local copies, waits for them, and re-layouts  1.86 us (3%)
    pallas_call x1, Pallas kernels, encode(): pl.pallas_call(functools.partial(kernel, h_count, w_count, rows1), name='...  55.7 us
    reshape x1, local copies, waits for them, and re-layouts, encode(): return jnp.transpose(out.reshape(rows3, G, N, 128), (2, 0, 1, 3))  1.86 us

profile of v6, /device:TPU:0, one launch (start us, length us, event | category | flops | bytes accessed | tf_op | source)
XLA Modules:
  0.0 57.5 jit_solution(18231698277968359370)
XLA Ops:
  0.0 55.7 %encoder.1 = bf16[16,2,16,16,128]{4,3,2,1,0:T(8,128)(2,1)S(1)} custom-call(bf16[16,1024,128]{2,1,0:T(8,128)(2,1)} %bitcast.15, bf16[2048,36]{1,0:T(8,128)(2,1)} %constant.2.clone.sel, bf16[9,4,32]{2,1,0:T(4,128)(2,1)} %bitcast.16, f32[1,32]{1,0:T(1,128)} %bitcast.17, bf16[3,3,32,32]{3,2,1,0:T(8,128)(2,1)} %rw1.1, f32[1,32]{1,0:T(1,128)} %bitcast.18, ...), custom_call_target="tpu_custom_call" | custom-call | flops 9965666304 | bytes 7340032 | tf_op jit(solution)/shard_map/encoder/pallas_call | solution.py:481
  55.7 1.9 %copy.17 = bf16[32,16,16,128]{3,1,0,2:T(8,128)(2,1)} copy(bf16[32,16,16,128]{3,2,1,0:T(8,128)(2,1)S(1)} %bitcast.14) | data formatting | bytes 4194304 | tf_op jit(solution)/shard_map/reshape | solution.py:501

commit v7 on v6

--- a/solution.py
+++ b/solution.py
@@ -225,6 +225,16 @@
 def row_blocks(rows, start, size):
     out = [(lo, min(lo + size, rows)) for lo in range(start, rows, size)]
     return out + [(lo, min(lo + size, start)) for lo in range(0, start, size)]
+
+
+BLOCKS = {
+    'y1': [(16, 96), (96, 128), (0, 16)],
+    'z1': [(24, 88), (88, 120), (120, 128), (0, 24)],
+    'y2': [(16, 40), (40, 56), (56, 64), (0, 16)],
+    'z2': [(24, 32), (32, 48), (48, 64), (0, 24)],
+    'y3': [(16, 24), (24, 32), (0, 16)],
+    'z3': [(4, 28), (28, 32), (0, 4)],
+}
 
 
 class Halo:
@@ -418,7 +428,7 @@
 
         unrolled((hi - lo) // per, step)
 
-    for is_edge, (lo, hi) in schedule(row_blocks(rows1, 16, 56), 1):
+    for is_edge, (lo, hi) in schedule(BLOCKS['y1'], 1):
         if is_edge:
             pv_halo.need_cols(lo - 1, hi)
             down1(lo, hi, 0, 1, 32)
@@ -433,6 +443,9 @@
         lhs = functools.partial(refine_lhs, stage, src)
         for is_edge, (lo, hi) in schedule(blocks, delay):
             if is_edge:
+                if dst_halo is None and lo == blocks[0][0]:
+                    for h in (pv_halo, y1_halo, z1_halo, y2_halo, z2_halo):
+                        h.finish()
                 src_halo.need_cols(lo - 1, hi + 1)
                 conv_rows(lhs, weight, bias, dst, lo, hi, [(0, 1), (G - 1, 1)], 16)
                 if dst_halo is not None:
@@ -455,15 +468,14 @@
                 conv_rows(lhs, weight, bias, dst, lo, hi, [(1, G - 1)], PAIRS)
                 dst_halo.send_cols(lo, hi, 0)
 
-    refine(1, y1, y1_halo, br1, tiled_bias(rb1), into_quads(z1), z1_halo, row_blocks(rows1, 24, 56), 1)
-    down(z1, z1_halo, bw2, tiled_bias(db2), into_pairs(y2, 1), y2_halo, row_blocks(rows2, 16, 24), 1)
-    refine(2, y2, y2_halo, br2, tiled_bias(rb2), into_quads(z2), z2_halo, row_blocks(rows2, 24, 24), 1)
-    down(z2, z2_halo, bw3, tiled_bias(db3), into_pairs(y3, 1), y3_halo, row_blocks(rows3, 16, 16), 4)
+    refine(1, y1, y1_halo, br1, tiled_bias(rb1), into_quads(z1), z1_halo, BLOCKS['z1'], 1)
+    down(z1, z1_halo, bw2, tiled_bias(db2), into_pairs(y2, 1), y2_halo, BLOCKS['y2'], 1)
+    refine(2, y2, y2_halo, br2, tiled_bias(rb2), into_quads(z2), z2_halo, BLOCKS['z2'], 1)
+    down(z2, z2_halo, bw3, tiled_bias(db3), into_pairs(y3, 1), y3_halo, BLOCKS['y3'], 3)
     refine(3, y3, y3_halo, br3, tiled_bias(rb3), into_pairs(out, 0), None,
-           [(4, rows3 - 4), (rows3 - 4, rows3), (0, 4)], 3)
-
-    for h in (pv_halo, y1_halo, z1_halo, y2_halo, z2_halo, y3_halo):
-        h.finish()
+           BLOCKS['z3'], 3)
+
+    y3_halo.finish()
 
 
 def encode(h_count, w_count, images, *params):

time: 57.7 us -> 58.5 us (1.014)
  Pallas kernels: 55.7 us -> 56.5 us
    pallas_call x1, Pallas kernels: 55.7 us -> 56.5 us  [encode(): pl.pallas_call(functools.partial(kernel, h_count, w_count, rows1), name='...]
where the time goes in v7:
time: 58.5 us; the launch traced here: 58.4 us
  Pallas kernels  56.5 us (97%)
  local copies, waits for them, and re-layouts  1.86 us (3%)
    pallas_call x1, Pallas kernels, encode(): pl.pallas_call(functools.partial(kernel, h_count, w_count, rows1), name='...  56.5 us
    reshape x1, local copies, waits for them, and re-layouts, encode(): return jnp.transpose(out.reshape(rows3, G, N, 128), (2, 0, 1, 3))  1.86 us

profile of v7, /device:TPU:0, one launch (start us, length us, event | category | flops | bytes accessed | tf_op | source)
XLA Modules:
  0.0 58.4 jit_solution(9047357643246974397)
XLA Ops:
  0.0 56.5 %encoder.1 = bf16[16,2,16,16,128]{4,3,2,1,0:T(8,128)(2,1)S(1)} custom-call(bf16[16,1024,128]{2,1,0:T(8,128)(2,1)} %bitcast.15, bf16[2048,36]{1,0:T(8,128)(2,1)} %constant.2.clone.sel, bf16[9,4,32]{2,1,0:T(4,128)(2,1)} %bitcast.16, f32[1,32]{1,0:T(1,128)} %bitcast.17, bf16[3,3,32,32]{3,2,1,0:T(8,128)(2,1)} %rw1.1, f32[1,32]{1,0:T(1,128)} %bitcast.18, ...), custom_call_target="tpu_custom_call" | custom-call | flops 9965666304 | bytes 7340032 | tf_op jit(solution)/shard_map/encoder/pallas_call | solution.py:493
  56.5 1.9 %copy.17 = bf16[32,16,16,128]{3,1,0,2:T(8,128)(2,1)} copy(bf16[32,16,16,128]{3,2,1,0:T(8,128)(2,1)S(1)} %bitcast.14) | data formatting | bytes 4194304 | tf_op jit(solution)/shard_map/reshape | solution.py:513

commit v8 on v6

--- a/solution.py
+++ b/solution.py
@@ -15,7 +15,7 @@
 TILES = 4
 DOWN1_ROWS = 8
 PAIRS = 4
-UNROLL = 0
+UNROLL = 1
 MESH = pl.DeviceIdType.MESH
 
 

time: 57.7 us -> 60.6 us (1.050)
  Pallas kernels: 55.7 us -> 58.6 us
    pallas_call x1, Pallas kernels: 55.7 us -> 58.6 us  [encode(): pl.pallas_call(functools.partial(kernel, h_count, w_count, rows1), name='...]
where the time goes in v8:
time: 60.6 us; the launch traced here: 60.5 us
  Pallas kernels  58.6 us (97%)
  local copies, waits for them, and re-layouts  1.86 us (3%)
    pallas_call x1, Pallas kernels, encode(): pl.pallas_call(functools.partial(kernel, h_count, w_count, rows1), name='...  58.6 us
    reshape x1, local copies, waits for them, and re-layouts, encode(): return jnp.transpose(out.reshape(rows3, G, N, 128), (2, 0, 1, 3))  1.86 us

profile of v8, /device:TPU:0, one launch (start us, length us, event | category | flops | bytes accessed | tf_op | source)
XLA Modules:
  0.0 60.5 jit_solution(4546818470507380737)
XLA Ops:
  0.0 58.6 %encoder.1 = bf16[16,2,16,16,128]{4,3,2,1,0:T(8,128)(2,1)S(1)} custom-call(bf16[16,1024,128]{2,1,0:T(8,128)(2,1)} %bitcast.15, bf16[2048,36]{1,0:T(8,128)(2,1)} %constant.2.clone.sel, bf16[9,4,32]{2,1,0:T(4,128)(2,1)} %bitcast.16, f32[1,32]{1,0:T(1,128)} %bitcast.17, bf16[3,3,32,32]{3,2,1,0:T(8,128)(2,1)} %rw1.1, f32[1,32]{1,0:T(1,128)} %bitcast.18, ...), custom_call_target="tpu_custom_call" | custom-call | flops 9965666304 | bytes 7340032 | tf_op jit(solution)/shard_map/encoder/pallas_call | solution.py:481
  58.6 1.9 %copy.17 = bf16[32,16,16,128]{3,1,0,2:T(8,128)(2,1)} copy(bf16[32,16,16,128]{3,2,1,0:T(8,128)(2,1)S(1)} %bitcast.14) | data formatting | bytes 4194304 | tf_op jit(solution)/shard_map/reshape | solution.py:501

commit v9 on v6

--- a/solution.py
+++ b/solution.py
@@ -13,7 +13,7 @@
 N = 16
 G = 16
 TILES = 4
-DOWN1_ROWS = 8
+DOWN1_ROWS = 16
 PAIRS = 4
 UNROLL = 0
 MESH = pl.DeviceIdType.MESH
@@ -416,9 +416,9 @@
                     y1[pairs, :, 1 + 2 * (q0 + q) + half] = v[:, :, q]
             return carry
 
-        unrolled((hi - lo) // per, step)
-
-    for is_edge, (lo, hi) in schedule(row_blocks(rows1, 16, 56), 1):
+        lax.fori_loop(0, (hi - lo) // per, step, 0)
+
+    for is_edge, (lo, hi) in schedule([(16, 80), (80, 128), (0, 16)], 1):
         if is_edge:
             pv_halo.need_cols(lo - 1, hi)
             down1(lo, hi, 0, 1, 32)
@@ -433,6 +433,9 @@
         lhs = functools.partial(refine_lhs, stage, src)
         for is_edge, (lo, hi) in schedule(blocks, delay):
             if is_edge:
+                if dst_halo is None and lo == blocks[0][0]:
+                    for h in (pv_halo, y1_halo, z1_halo, y2_halo, z2_halo):
+                        h.finish()
                 src_halo.need_cols(lo - 1, hi + 1)
                 conv_rows(lhs, weight, bias, dst, lo, hi, [(0, 1), (G - 1, 1)], 16)
                 if dst_halo is not None:
@@ -462,8 +465,7 @@
     refine(3, y3, y3_halo, br3, tiled_bias(rb3), into_pairs(out, 0), None,
            [(4, rows3 - 4), (rows3 - 4, rows3), (0, 4)], 3)
 
-    for h in (pv_halo, y1_halo, z1_halo, y2_halo, z2_halo, y3_halo):
-        h.finish()
+    y3_halo.finish()
 
 
 def encode(h_count, w_count, images, *params):

time: 57.7 us -> 58.7 us (1.017)
  Pallas kernels: 55.7 us -> 56.7 us
    pallas_call x1, Pallas kernels: 55.7 us -> 56.7 us  [encode(): pl.pallas_call(functools.partial(kernel, h_count, w_count, rows1), name='...]
where the time goes in v9:
time: 58.7 us; the launch traced here: 58.6 us
  Pallas kernels  56.7 us (97%)
  local copies, waits for them, and re-layouts  1.86 us (3%)
    pallas_call x1, Pallas kernels, encode(): pl.pallas_call(functools.partial(kernel, h_count, w_count, rows1), name='...  56.7 us
    reshape x1, local copies, waits for them, and re-layouts, encode(): return jnp.transpose(out.reshape(rows3, G, N, 128), (2, 0, 1, 3))  1.86 us

profile of v9, /device:TPU:0, one launch (start us, length us, event | category | flops | bytes accessed | tf_op | source)
XLA Modules:
  0.0 58.6 jit_solution(9265474914117445160)
XLA Ops:
  0.0 56.7 %encoder.1 = bf16[16,2,16,16,128]{4,3,2,1,0:T(8,128)(2,1)S(1)} custom-call(bf16[16,1024,128]{2,1,0:T(8,128)(2,1)} %bitcast.15, bf16[2048,36]{1,0:T(8,128)(2,1)} %constant.2.clone.sel, bf16[9,4,32]{2,1,0:T(4,128)(2,1)} %bitcast.16, f32[1,32]{1,0:T(1,128)} %bitcast.17, bf16[3,3,32,32]{3,2,1,0:T(8,128)(2,1)} %rw1.1, f32[1,32]{1,0:T(1,128)} %bitcast.18, ...), custom_call_target="tpu_custom_call" | custom-call | flops 9965666304 | bytes 7340032 | tf_op jit(solution)/shard_map/encoder/pallas_call | solution.py:483
  56.7 1.9 %copy.17 = bf16[32,16,16,128]{3,1,0,2:T(8,128)(2,1)} copy(bf16[32,16,16,128]{3,2,1,0:T(8,128)(2,1)S(1)} %bitcast.14) | data formatting | bytes 4194304 | tf_op jit(solution)/shard_map/reshape | solution.py:503

commit v10 on v6

--- a/solution.py
+++ b/solution.py
@@ -13,7 +13,7 @@
 N = 16
 G = 16
 TILES = 4
-DOWN1_ROWS = 8
+DOWN1_ROWS = 4
 PAIRS = 4
 UNROLL = 0
 MESH = pl.DeviceIdType.MESH

time: 57.7 us -> 57.7 us (level)
  no operation moved by 1% of the time
where the time goes in v10:
time: 57.7 us; the launch traced here: 57.5 us
  Pallas kernels  55.7 us (97%)
  local copies, waits for them, and re-layouts  1.86 us (3%)
    pallas_call x1, Pallas kernels, encode(): pl.pallas_call(functools.partial(kernel, h_count, w_count, rows1), name='...  55.7 us
    reshape x1, local copies, waits for them, and re-layouts, encode(): return jnp.transpose(out.reshape(rows3, G, N, 128), (2, 0, 1, 3))  1.86 us

profile of v10, /device:TPU:0, one launch (start us, length us, event | category | flops | bytes accessed | tf_op | source)
XLA Modules:
  0.0 57.5 jit_solution(479520121914673628)
XLA Ops:
  0.0 55.7 %encoder.1 = bf16[16,2,16,16,128]{4,3,2,1,0:T(8,128)(2,1)S(1)} custom-call(bf16[16,1024,128]{2,1,0:T(8,128)(2,1)} %bitcast.15, bf16[2048,36]{1,0:T(8,128)(2,1)} %constant.2.clone.sel, bf16[9,4,32]{2,1,0:T(4,128)(2,1)} %bitcast.16, f32[1,32]{1,0:T(1,128)} %bitcast.17, bf16[3,3,32,32]{3,2,1,0:T(8,128)(2,1)} %rw1.1, f32[1,32]{1,0:T(1,128)} %bitcast.18, ...), custom_call_target="tpu_custom_call" | custom-call | flops 9965666304 | bytes 7340032 | tf_op jit(solution)/shard_map/encoder/pallas_call | solution.py:481
  55.7 1.9 %copy.17 = bf16[32,16,16,128]{3,1,0,2:T(8,128)(2,1)} copy(bf16[32,16,16,128]{3,2,1,0:T(8,128)(2,1)S(1)} %bitcast.14) | data formatting | bytes 4194304 | tf_op jit(solution)/shard_map/reshape | solution.py:501
